TPU v7x, 16 devices: a whole 2x2x2 slice. The times are simulated.
16 devices in a mesh: dp: 16 (over z, y, x, core).
Axes of the slice: x: 2, y: 2, z: 2, core: 2. Of those that a mesh axis runs over, the one named last changes fastest.
Arguments:
- token_ids: int32 [32, 384], P('dp')
- target_ids: int32 [32, 384], P('dp')
- st_wte: float32 [3, 40478, 768], P(None, None, 'dp')
- st_wpe: float32 [3, 514, 768], P(None, None, 'dp')
- st_qkv: float32 [3, 2, 768, 3, 12, 64], P(None, None, 'dp')
- st_proj: float32 [3, 2, 12, 64, 768], P(None, None, None, None, 'dp')
- st_up: float32 [3, 2, 768, 3072], P(None, None, 'dp')
- st_down: float32 [3, 2, 3072, 768], P(None, None, 'dp')
- st_vec: float32 [3, 2, 9984], P(None, None, 'dp')
- st_lnf: float32 [3, 2, 768], P(None, None, 'dp')
Outputs:
- output 1: float32 [], replicated
- output 2: float32 [3, 40478, 768], P(None, None, 'dp')
- output 3: float32 [3, 514, 768], P(None, None, 'dp')
- output 4: float32 [3, 2, 768, 3, 12, 64], P(None, None, 'dp')
- output 5: float32 [3, 2, 12, 64, 768], P(None, None, None, None, 'dp')
- output 6: float32 [3, 2, 768, 3072], P(None, None, 'dp')
- output 7: float32 [3, 2, 3072, 768], P(None, None, 'dp')
- output 8: float32 [3, 2, 9984], P(None, None, 'dp')
- output 9: float32 [3, 2, 768], P(None, None, 'dp')
All inputs are finite; a program needn't handle non-finite values.
Results may differ from a plain program's by a relative error of at most 0.00221679.
Values are sent between devices in bfloat16 or wider.
A program may use at most 1 GiB of HBM per device.

v0:
```python
import jax
import jax.numpy as jnp
from jax import lax
from jax.sharding import PartitionSpec as P

NORM_EPS = 1e-5
LEARN_RATE = 3e-3
BETA_ONE = 0.9
BETA_TWO = 0.95
ADAM_EPS = 1e-8
WEIGHT_DECAY = 0.1
CLIP_NORM = 1.0
ADAM_STEP = 10
DECAYS = (WEIGHT_DECAY,) * 6 + (0.0, 0.0)
LAYER_AXES = (0, 2, 0, 0, 0)


def layer_norm(residual, gain, bias):
    mean_val = jnp.mean(residual, axis=-1, keepdims=True)
    centered = residual - mean_val
    variance = jnp.mean(centered * centered, axis=-1, keepdims=True)
    return centered * lax.rsqrt(variance + NORM_EPS) * gain.astype(jnp.float32) + bias.astype(jnp.float32)


def block(residual, weights):
    qkv_w, proj_w, up_w, down_w, layer_vec = weights
    seq_len, d_model = residual.shape[1], residual.shape[2]
    num_heads, head_dim = proj_w.shape[0], proj_w.shape[1]
    offset = 4 * d_model + up_w.shape[1]
    ln_par = layer_vec[offset + d_model:].reshape(4, d_model)
    normed_in = layer_norm(residual, ln_par[0], ln_par[1]).astype(jnp.bfloat16)
    qkv_all = jnp.einsum('bsd,dthk->tbshk', normed_in, qkv_w, preferred_element_type=jnp.float32)
    qkv_all = (qkv_all + layer_vec[:3 * d_model].astype(jnp.float32).reshape(3, 1, 1, num_heads, head_dim)).astype(jnp.bfloat16)
    scores = jnp.einsum('bqhk,bshk->bhqs', qkv_all[0], qkv_all[1], preferred_element_type=jnp.float32) * head_dim ** -0.5
    rows_iota = lax.broadcasted_iota(jnp.int32, (seq_len, seq_len), 0)
    cols_iota = lax.broadcasted_iota(jnp.int32, (seq_len, seq_len), 1)
    scores = jnp.where(rows_iota >= cols_iota, scores, -1e30)
    attn_prob = jax.nn.softmax(scores, axis=-1).astype(jnp.bfloat16)
    mixed = jnp.einsum('bhqs,bshk->bqhk', attn_prob, qkv_all[2], preferred_element_type=jnp.float32).astype(jnp.bfloat16)
    residual = residual + jnp.einsum('cril,ile->cre', mixed, proj_w, preferred_element_type=jnp.float32) + layer_vec[3 * d_model:4 * d_model].astype(jnp.float32)
    normed_mid = layer_norm(residual, ln_par[2], ln_par[3]).astype(jnp.bfloat16)
    hidden = jax.nn.relu(jnp.einsum('bsd,df->bsf', normed_mid, up_w, preferred_element_type=jnp.float32) + layer_vec[4 * d_model:offset].astype(jnp.float32)).astype(jnp.bfloat16)
    return residual + jnp.einsum('bsf,fd->bsd', hidden, down_w, preferred_element_type=jnp.float32) + layer_vec[offset:offset + d_model].astype(jnp.float32)


def final_norm(residual, lnf_c):
    return layer_norm(residual, lnf_c[0], lnf_c[1]).astype(jnp.bfloat16)


def head_loss(normed, target_ids, head_w, inv_tokens):
    vocab_size, d_model = head_w.shape

    def row_step(carry, row):
        grad_acc, loss_acc = carry
        h_row, t_row = row
        logits = jnp.einsum('sd,vd->sv', h_row, head_w, preferred_element_type=jnp.float32)
        shifted = logits - jnp.max(logits, axis=-1, keepdims=True)
        exp_shift = jnp.exp(shifted)
        sum_exp = jnp.sum(exp_shift, axis=-1, keepdims=True)
        is_target = lax.broadcasted_iota(jnp.int32, logits.shape, 1) == t_row[:, None]
        picked = jnp.sum(jnp.where(is_target, shifted, 0.0), axis=-1)
        loss_acc = loss_acc + jnp.sum(jnp.log(sum_exp[:, 0]) - picked) * inv_tokens
        d_logits = ((exp_shift / sum_exp - is_target.astype(jnp.float32)) * inv_tokens).astype(jnp.bfloat16)
        grad_acc = grad_acc + jnp.einsum('sv,sd->vd', d_logits, h_row, preferred_element_type=jnp.float32)
        d_row = jnp.einsum('sv,vd->sd', d_logits, head_w, preferred_element_type=jnp.float32)
        return (grad_acc, loss_acc), d_row

    init_carry = (jnp.zeros((vocab_size, d_model), jnp.float32), jnp.zeros((), jnp.float32))
    (grad_head, loss_part), d_normed = lax.scan(row_step, init_carry, (normed, target_ids))
    return grad_head, loss_part, d_normed


def adam_update(state, grad, decay):
    moment = BETA_ONE * state[1] + (1.0 - BETA_ONE) * grad
    second = BETA_TWO * state[2] + (1.0 - BETA_TWO) * grad * grad
    m_hat = moment / (1.0 - BETA_ONE ** ADAM_STEP)
    v_hat = second / (1.0 - BETA_TWO ** ADAM_STEP)
    master = state[0] * (1.0 - LEARN_RATE * decay) - LEARN_RATE * m_hat / (jnp.sqrt(v_hat) + ADAM_EPS)
    return jnp.stack([master, moment, second])


def solution(mesh):
    n_dev = mesh.shape['dp']
    row_spec = P('dp', None)
    state_specs = (P(None, None, 'dp'), P(None, None, 'dp'), P(None, None, 'dp', None, None, None), P(None, None, None, None, 'dp'), P(None, None, 'dp', None), P(None, None, 'dp', None), P(None, None, 'dp'), P(None, None, 'dp'))

    def collect(local, axis):
        return lax.all_gather(local.astype(jnp.bfloat16), 'dp', axis=axis, tiled=True)

    def spread(full, axis):
        return lax.psum_scatter(full.astype(jnp.float32), 'dp', scatter_dimension=axis, tiled=True)

    def train_step(token_ids, target_ids, st_wte, st_wpe, st_qkv, st_proj, st_up, st_down, st_vec, st_lnf):
        num_layers = st_qkv.shape[1]
        batch_dev, seq_len = token_ids.shape
        vocab_size = st_wte.shape[1]
        pos_rows = st_wpe.shape[1]
        inv_tokens = 1.0 / (batch_dev * seq_len * n_dev)
        layer_states = (st_qkv, st_proj, st_up, st_down, st_vec)

        def layer_weights(layer):
            return tuple(collect(state[0, layer], axis) for state, axis in zip(layer_states, LAYER_AXES))

        wte_c = collect(st_wte[0], 1)
        wpe_c = collect(st_wpe[0], 1)
        residual = jnp.take(wte_c, token_ids, axis=0).astype(jnp.float32) + wpe_c[2:2 + seq_len].astype(jnp.float32)
        saved = []
        for layer in range(num_layers):
            saved.append(residual)
            residual = block(residual, layer_weights(layer))
        lnf_c = collect(st_lnf[0], 1)
        normed, norm_back = jax.vjp(final_norm, residual, lnf_c)
        head_w = collect(st_wte[0], 1)
        grad_head, loss_part, d_normed = head_loss(normed, target_ids, head_w, inv_tokens)
        d_resid, d_lnf = norm_back(d_normed.astype(jnp.bfloat16))
        layer_grads = [None] * num_layers
        for layer in reversed(range(num_layers)):
            _, block_back = jax.vjp(block, saved[layer], layer_weights(layer))
            d_resid, d_weights = block_back(d_resid)
            layer_grads[layer] = tuple(spread(grad, axis) for grad, axis in zip(d_weights, LAYER_AXES))
        d_model = d_resid.shape[-1]
        lookup_grad = jax.ops.segment_sum(d_resid.reshape(-1, d_model), token_ids.reshape(-1), num_segments=vocab_size)
        pos_grad = jnp.pad(jnp.sum(d_resid, axis=0), ((2, pos_rows - 2 - seq_len), (0, 0)))
        grads = [spread(grad_head + lookup_grad, 1), spread(pos_grad, 1)]
        for kind in range(5):
            grads.append(jnp.stack([layer_grads[layer][kind] for layer in range(num_layers)]))
        grads.append(spread(d_lnf, 1))
        local_sq = sum(jnp.sum(grad * grad) for grad in grads)
        grad_norm = jnp.sqrt(lax.psum(local_sq, 'dp'))
        clip_coef = jnp.minimum(1.0, CLIP_NORM / (grad_norm + 1e-6))
        states = (st_wte, st_wpe, st_qkv, st_proj, st_up, st_down, st_vec, st_lnf)
        new_states = tuple(adam_update(state, grad * clip_coef, decay) for state, grad, decay in zip(states, grads, DECAYS))
        loss = lax.psum(loss_part, 'dp')
        return (loss,) + new_states

    return jax.shard_map(train_step, mesh=mesh, in_specs=(row_spec, row_spec) + state_specs, out_specs=(P(),) + state_specs, check_vma=False)
```

profile of v0, /device:TPU:0, one launch (start us, length us, event | category | flops | bytes accessed | tf_op | source)
XLA Modules:
  0.0 2630.9 jit_solution(2971521888139411102)
XLA Ops:
  26.5 36.1 %all-reduce.33 = (bf16[9984]{0:T(1024)(128)(2,1)S(1)}, bf16[9984]{0:T(1024)(128)(2,1)S(1)}) all-reduce(bf16[9984]{0:T(1024)(128)(2,1)S(1)} %dynamic-update-slice, bf16[9984]{0:T(1024)(128)(2,1)S(1)} %dynamic-update-slice.1), channel_id=4, replica_groups=mesh['dp'=16] {'dp'}, use_global_device_ids=true, to_apply=%add.27 | all-reduce | flops 19968 | bytes 79872
  68.0 17.4 all-gather.1
  88.8 11.9 all-gather.12
  101.5 144.1 %all-gather.23.cloned.1.call-done = bf16[1,40478,768]{1,2,0:T(8,128)(2,1)} async-done(((bf16[1,40478,48]{1,2,0:T(8,128)(2,1)}), bf16[1,40478,768]{1,2,0:T(8,128)(2,1)}) %all-gather.23.cloned.1.call-update) | async-done | bytes 62174224 | tf_op jit(solution)/shard_map/all_gather | solution.py:88
  245.5 80.4 %copy.134 = bf16[1,40478,768]{2,1,0:T(8,128)(2,1)} copy(bf16[1,40478,768]{1,2,0:T(8,128)(2,1)} %all-gather.23.cloned.1.call-done) | data formatting | bytes 124348416 | tf_op jit(solution)/shard_map/all_gather | solution.py:88
  375.1 12.5 fusion.101
  387.6 15.6 all-gather.31.cloned.1.call-done
  413.2 38.4 %all-gather.33.cloned.1.call-done = bf16[1,1,768,3,12,64]{5,2,4,3,1,0:T(8,128)(2,1)} async-done(((bf16[1,1,48,3,12,64]{5,2,4,3,1,0:T(8,128)(2,1)}), bf16[1,1,768,3,12,64]{5,2,4,3,1,0:T(8,128)(2,1)}) %all-gather.33.cloned.1.call-update) | async-done | bytes 3538960 | tf_op jit(solution)/shard_map/all_gather | solution.py:88
  491.7 30.3 %all-gather.37.cloned.1.call-done = bf16[1,1,768,3072]{3,2,1,0:T(8,128)(2,1)} async-done(((bf16[1,1,48,3072]{3,2,1,0:T(8,128)(2,1)}), bf16[1,1,768,3072]{3,2,1,0:T(8,128)(2,1)}) %all-gather.37.cloned.1.call-update) | async-done | bytes 4718608 | tf_op jit(solution)/shard_map/all_gather | solution.py:88
  532.7 28.8 %all-gather.39.cloned.1.call-done = bf16[1,1,3072,768]{3,2,1,0:T(8,128)(2,1)} async-done(((bf16[1,1,192,768]{3,2,1,0:T(8,128)(2,1)}), bf16[1,1,3072,768]{3,2,1,0:T(8,128)(2,1)}) %all-gather.39.cloned.1.call-update) | async-done | bytes 4718608 | tf_op jit(solution)/shard_map/all_gather | solution.py:88
  572.4 414.1 %while.15 = (s32[]{:T(128)}, f32[40478,768]{1,0:T(8,128)}, f32[]{:T(128)}, bf16[2,384,768]{2,1,0:T(8,128)(2,1)S(1)}, bf16[2,384,768]{2,1,0:T(8,128)(2,1)}, /*ind...) while((s32[]{:T(128)}, f32[40478,768]{1,0:T(8,128)}, ...), condition=%wide.region_19.20_spmd.clone, body=%wide.region_14.0_spmd.clone.sunk | while | flops 71997734912 | bytes 624152256 | solution.py:69
  572.9 54.1 %fusion.324 = (f32[384]{0:T(512)S(1)}, f32[384,40478]{0,1:T(8,128)}) fusion(bf16[40478,768]{1,0:T(8,128)(2,1)} %get-tuple-element.303, bf16[2,384,768]{2,1,0:T(8,128)(2,1)} %get-tuple-element.302, s32[]{:T(128)} %get-tuple-element.288), kind=kOutput, calls=%fused_computation.407.clone.2 | convolution fusion | flops 23890438144 | bytes 124943360 | tf_op jit(solution)/shard_map/while/body/eval_jaxpr/sd,vd->sv/dot_general | solution.py:56
  627.6 20.9 select_reduce_fusion.2
  648.6 43.2 %fusion.325 = bf16[2,384,768]{2,1,0:T(8,128)(2,1)S(1)} fusion(bf16[2,384,768]{2,1,0:T(8,128)(2,1)S(1)} %get-tuple-element.291, s32[]{:T(128)} %get-tuple-element.288, bf16[40478,768]{1,0:T(8,128)(2,1)} %get-tuple-element.303, f32[384,40478]{0,1:T(8,128)} %get-tuple-element.274, s32[384]{0:T(512)S(1)} %dynamic-slice_reduce_fusion.2, ...), kind=kOutput, calls=%fused_computation.8.clone.2 | convolution fusion | flops 23983699968 | bytes 125534208 | tf_op jit(solution)/shard_map/while/body/eval_jaxpr/sv,vd->sd/dot_general | solution.py:65
  691.7 67.7 %select_add_fusion.2 = f32[40478,768]{1,0:T(8,128)} fusion(f32[40478,768]{1,0:T(8,128)} %get-tuple-element.289, pred[]{:T(512)S(6)} %compare.30, bf16[2,384,768]{2,1,0:T(8,128)(2,1)} %get-tuple-element.302, s32[]{:T(128)} %get-tuple-element.288, f32[384,40478]{0,1:T(8,128)} %get-tuple-element.274, s32[384]{0:T(512)S(1)} %dynamic-slice_reduce_fusion.2, ...), kind=kOutput, calls=%fused_computation.2.clone.3 | convolution fusion | flops 24045875200 | bytes 311475712 | tf_op jit(solution)/shard_map/while/body/eval_jaxpr/sv,sd->vd/dot_general | solution.py:64
  760.6 53.8 %fusion.324 = (f32[384]{0:T(512)S(1)}, f32[384,40478]{0,1:T(8,128)}) fusion(bf16[40478,768]{1,0:T(8,128)(2,1)} %get-tuple-element.303, bf16[2,384,768]{2,1,0:T(8,128)(2,1)} %get-tuple-element.302, s32[]{:T(128)} %get-tuple-element.288), kind=kOutput, calls=%fused_computation.407.clone.2 | convolution fusion | flops 23890438144 | bytes 124943360 | tf_op jit(solution)/shard_map/while/body/eval_jaxpr/sd,vd->sv/dot_general | solution.py:56
  815.1 20.9 select_reduce_fusion.2
  836.0 43.2 %fusion.325 = bf16[2,384,768]{2,1,0:T(8,128)(2,1)S(1)} fusion(bf16[2,384,768]{2,1,0:T(8,128)(2,1)S(1)} %get-tuple-element.291, s32[]{:T(128)} %get-tuple-element.288, bf16[40478,768]{1,0:T(8,128)(2,1)} %get-tuple-element.303, f32[384,40478]{0,1:T(8,128)} %get-tuple-element.274, s32[384]{0:T(512)S(1)} %dynamic-slice_reduce_fusion.2, ...), kind=kOutput, calls=%fused_computation.8.clone.2 | convolution fusion | flops 23983699968 | bytes 125534208 | tf_op jit(solution)/shard_map/while/body/eval_jaxpr/sv,vd->sd/dot_general | solution.py:65
  879.2 106.0 %select_add_fusion.2 = f32[40478,768]{1,0:T(8,128)} fusion(f32[40478,768]{1,0:T(8,128)} %get-tuple-element.289, pred[]{:T(512)S(6)} %compare.30, bf16[2,384,768]{2,1,0:T(8,128)(2,1)} %get-tuple-element.302, s32[]{:T(128)} %get-tuple-element.288, f32[384,40478]{0,1:T(8,128)} %get-tuple-element.274, s32[384]{0:T(512)S(1)} %dynamic-slice_reduce_fusion.2, ...), kind=kOutput, calls=%fused_computation.2.clone.3 | convolution fusion | flops 24045875200 | bytes 311475712 | tf_op jit(solution)/shard_map/while/body/eval_jaxpr/sv,sd->vd/dot_general | solution.py:64
  1253.1 97.9 %scatter_fusion = f32[40478,768]{1,0:T(8,128)} fusion(f32[40478,768]{1,0:T(8,128)} %get-tuple-element.49, s32[768]{0:T(1024)S(1)} %reshape.754, f32[768,768]{1,0:T(8,128)S(1)} %bitcast.561), kind=kCustom, calls=%fused_computation.1 | custom fusion | flops 589824 | bytes 7080960 | tf_op jit(solution)/shard_map/scatter-add | solution.py:122
  1351.0 121.3 %copy.195 = f32[40478,768]{0,1:T(8,128)} copy(f32[40478,768]{1,0:T(8,128)} %scatter_fusion) | data formatting | bytes 248696832
  1480.7 38.2 %reduce-scatter.18.cloned.1.call-done = f32[48,3,12,64]{3,0,2,1:T(8,128)} async-done(((f32[768,3,12,64]{3,0,2,1:T(8,128)}), f32[48,3,12,64]{3,0,2,1:T(8,128)}) %reduce-scatter.18.cloned.1.call-update) | async-done | bytes 442384 | tf_op jit(solution)/shard_map/reduce_scatter | solution.py:91
  1519.0 102.5 %reduce-scatter.20.cloned.1.call-done = f32[48,3,12,64]{3,0,2,1:T(8,128)} async-done(((f32[768,3,12,64]{3,0,2,1:T(8,128)}), f32[48,3,12,64]{3,0,2,1:T(8,128)}) %reduce-scatter.20.cloned.1.call-update) | async-done | bytes 442384 | tf_op jit(solution)/shard_map/reduce_scatter | solution.py:91
  1624.0 81.5 %reduce-scatter.32.cloned.1.call-done = f32[192,768]{1,0:T(8,128)} async-done(((f32[3072,768]{1,0:T(8,128)}), f32[192,768]{1,0:T(8,128)}) %reduce-scatter.32.cloned.1.call-update) | async-done | bytes 589840 | tf_op jit(solution)/shard_map/reduce_scatter | solution.py:91
  1705.5 84.0 %reduce-scatter.30.cloned.1.call-done = f32[192,768]{1,0:T(8,128)} async-done(((f32[3072,768]{1,0:T(8,128)}), f32[192,768]{1,0:T(8,128)}) %reduce-scatter.30.cloned.1.call-update) | async-done | bytes 589840 | tf_op jit(solution)/shard_map/reduce_scatter | solution.py:91
  1791.7 82.0 %reduce-scatter.26.cloned.1.call-done = f32[48,3072]{1,0:T(8,128)} async-done(((f32[768,3072]{1,0:T(8,128)}), f32[48,3072]{1,0:T(8,128)}) %reduce-scatter.26.cloned.1.call-update) | async-done | bytes 589840 | tf_op jit(solution)/shard_map/reduce_scatter | solution.py:91
  1873.7 84.0 %reduce-scatter.28.cloned.1.call-done = f32[48,3072]{1,0:T(8,128)} async-done(((f32[768,3072]{1,0:T(8,128)}), f32[48,3072]{1,0:T(8,128)}) %reduce-scatter.28.cloned.1.call-update) | async-done | bytes 589840 | tf_op jit(solution)/shard_map/reduce_scatter | solution.py:91
  1959.9 550.0 %reduce-scatter.34.cloned.1.call-done = f32[48,40478]{1,0:T(8,128)} async-done(((f32[768,40478]{1,0:T(8,128)}), f32[48,40478]{1,0:T(8,128)}) %reduce-scatter.34.cloned.1.call-update) | async-done | bytes 7771792
  2509.9 13.7 copy.196
  2539.3 32.4 %all-reduce.31 = (f32[]{:T(128)}, f32[]{:T(128)}) all-reduce(f32[]{:T(128)} %get-tuple-element.48, f32[]{:T(128)S(6)} %add.517), channel_id=1, replica_groups=mesh['dp'=16] {'dp'}, use_global_device_ids=true, to_apply=%region_20.21 | all-reduce | flops 2 | bytes 16 | tf_op jit(solution)/shard_map/psum | solution.py:133
  2593.1 16.2 fusion.31
  2609.4 14.5 pad_maximum_fusion
  (587 shorter events, 463.4 us)
Async XLA Ops:
  7.2 238.4 %all-gather.23.cloned.1.call-start = ((), (), s32[]{:S(2)}) async-start(), calls=%async_computation.19 | async-start | bytes 66220032 | tf_op jit(solution)/shard_map/all_gather | solution.py:88
  12.8 321.2 %all-gather.25.cloned.1.call-start = ((), (), s32[]{:S(2)}) async-start(), calls=%async_computation.20 | async-start | bytes 7520256 | tf_op jit(solution)/shard_map/all_gather | solution.py:88
  16.8 351.1 %all-gather.27.cloned.1.call-start = ((), (), s32[]{:S(2)}) async-start(), calls=%async_computation.21 | async-start | bytes 2506752 | tf_op jit(solution)/shard_map/all_gather | solution.py:88
  18.5 356.5 %all-gather.29.cloned.1.call-start = ((), (), s32[]{:S(2)}) async-start(), calls=%async_computation.22 | async-start | bytes 5013504 | tf_op jit(solution)/shard_map/all_gather | solution.py:88
  21.9 381.3 %all-gather.31.cloned.1.call-start = ((), (), s32[]{:S(2)}) async-start(), calls=%async_computation.23 | async-start | bytes 5013504 | tf_op jit(solution)/shard_map/all_gather | solution.py:88
  23.0 428.6 %all-gather.33.cloned.1.call-start = ((), (), s32[]{:S(2)}) async-start(), calls=%async_computation.24 | async-start | bytes 7520256 | tf_op jit(solution)/shard_map/all_gather | solution.py:88
  23.6 461.5 %all-gather.35.cloned.1.call-start = ((), (), s32[]{:S(2)}) async-start(), calls=%async_computation.25 | async-start | bytes 2506752 | tf_op jit(solution)/shard_map/all_gather | solution.py:88
  24.3 497.7 %all-gather.37.cloned.1.call-start = ((), (), s32[]{:S(2)}) async-start(), calls=%async_computation.26 | async-start | bytes 5013504 | tf_op jit(solution)/shard_map/all_gather | solution.py:88
  25.1 536.5 %all-gather.39.cloned.1.call-start = ((), (), s32[]{:S(2)}) async-start(), calls=%async_computation.27 | async-start | bytes 5013504 | tf_op jit(solution)/shard_map/all_gather | solution.py:88
  25.8 1446.5 %reduce-scatter.38.cloned.1.call-start = ((), (), s32[]{:S(2)}) async-start(), calls=%async_computation.30 | async-start | bytes 417792
  25.9 342.0 %copy-start.85 = (pred[2,384]{1,0:T(4,128)(4,1)}, pred[2,384]{1,0:T(4,128)(4,1)S(1)}, u32[]{:S(2)}) copy-start(pred[2,384]{1,0:T(4,128)(4,1)S(1)} %compare_and_fusion) | copy-start | bytes 2308
  86.0 281.9 %copy-start.4 = (f32[384,768]{1,0:T(8,128)}, f32[384,768]{1,0:T(8,128)S(1)}, u32[]{:S(2)}) copy-start(f32[384,768]{1,0:T(8,128)S(1)} %copy.135) | copy-start | bytes 3538948
  101.5 469.5 %copy-start.67 = (f32[768]{0:T(1024)}, f32[768]{0:T(1024)S(1)}, u32[]{:S(2)}) copy-start(f32[768]{0:T(1024)S(1)} %get-tuple-element.128) | copy-start | bytes 9220
  101.5 224.4 %copy-start.130 = (s32[1024]{0:T(1024)S(1)}, s32[1024]{0:T(1024)}, u32[]{:S(2)}) copy-start(s32[1024]{0:T(1024)} %pad_clamp_fusion) | copy-start | bytes 12292
  490.0 71.5 %copy-start.10 = (f32[2,384,768]{2,1,0:T(8,128)}, f32[2,384,768]{2,1,0:T(8,128)S(1)}, u32[]{:S(2)}) copy-start(f32[2,384,768]{2,1,0:T(8,128)S(1)} %get-tuple-element.204) | copy-start | bytes 7077892
  572.4 414.2 %copy-start.1 = (f32[2,384,768]{2,1,0:T(8,128)S(1)}, f32[2,384,768]{2,1,0:T(8,128)}, u32[]{:S(2)}) copy-start(f32[2,384,768]{2,1,0:T(8,128)} %copy-done) | copy-start | bytes 7077892
  572.4 414.2 %copy-start.66 = (f32[2,384]{1,0:T(2,128)S(1)}, f32[2,384]{1,0:T(2,128)}, u32[]{:S(2)}) copy-start(f32[2,384]{1,0:T(2,128)} %copy-done.65) | copy-start | bytes 9220
  691.7 67.7 %copy-start.57 = (f32[384]{0:T(512)S(1)}, f32[384]{0:T(512)}, u32[]{:S(2)}) copy-start(f32[384]{0:T(512)} %get-tuple-element.277) | copy-start | bytes 4612 | tf_op jit(solution)/shard_map/while
  879.2 106.0 %copy-start.57 = (f32[384]{0:T(512)S(1)}, f32[384]{0:T(512)}, u32[]{:S(2)}) copy-start(f32[384]{0:T(512)} %get-tuple-element.277) | copy-start | bytes 4612 | tf_op jit(solution)/shard_map/while
  1013.4 96.3 %copy-start.35 = (bf16[1,2,384,12,64]{2,4,3,1,0:T(8,128)(2,1)}, bf16[1,2,384,12,64]{2,4,3,1,0:T(8,128)(2,1)S(1)}, u32[]{:S(2)}) copy-start(bf16[1,2,384,12,64]{2,4,3,1,0:T(8,128)(2,1)S(1)} %fusion.182) | copy-start | bytes 3538948
  1117.0 356.8 %all-reduce.36.cloned.1.call-start = ((), (), s32[]{:S(2)}) async-start(), calls=%async_computation.31 | async-start | bytes 163840
  1161.9 315.3 %reduce-scatter.36.cloned.1.call-start = ((), (), s32[]{:S(2)}) async-start(), calls=%async_computation.29 | async-start | bytes 2088960
  1165.1 313.8 %reduce-scatter.24.cloned.1.call-start = ((), (), s32[]{:S(2)}) async-start(), calls=%async_computation.14 | async-start | bytes 5013504 | tf_op jit(solution)/shard_map/reduce_scatter | solution.py:91
  1170.6 308.3 %reduce-scatter.22.cloned.1.call-start = ((), (), s32[]{:S(2)}) async-start(), calls=%async_computation.13 | async-start | bytes 5013504 | tf_op jit(solution)/shard_map/reduce_scatter | solution.py:91
  1177.2 341.7 %reduce-scatter.18.cloned.1.call-start = ((), (), s32[]{:S(2)}) async-start(), calls=%async_computation.11 | async-start | bytes 15040512 | tf_op jit(solution)/shard_map/reduce_scatter | solution.py:91
  1189.6 431.9 %reduce-scatter.20.cloned.1.call-start = ((), (), s32[]{:S(2)}) async-start(), calls=%async_computation.12 | async-start | bytes 15040512 | tf_op jit(solution)/shard_map/reduce_scatter | solution.py:91
  1202.3 503.2 %reduce-scatter.32.cloned.1.call-start = ((), (), s32[]{:S(2)}) async-start(), calls=%async_computation.18 | async-start | bytes 10027008 | tf_op jit(solution)/shard_map/reduce_scatter | solution.py:91
  1214.4 575.1 %reduce-scatter.30.cloned.1.call-start = ((), (), s32[]{:S(2)}) async-start(), calls=%async_computation.17 | async-start | bytes 10027008 | tf_op jit(solution)/shard_map/reduce_scatter | solution.py:91
  1226.3 647.4 %reduce-scatter.26.cloned.1.call-start = ((), (), s32[]{:S(2)}) async-start(), calls=%async_computation.15 | async-start | bytes 10027008 | tf_op jit(solution)/shard_map/reduce_scatter | solution.py:91
  1238.8 718.9 %reduce-scatter.28.cloned.1.call-start = ((), (), s32[]{:S(2)}) async-start(), calls=%async_computation.16 | async-start | bytes 10027008 | tf_op jit(solution)/shard_map/reduce_scatter | solution.py:91
  1251.4 1258.5 %reduce-scatter.34.cloned.1.call-start = ((), (), s32[]{:S(2)}) async-start(), calls=%async_computation.28 | async-start | bytes 132440064
  2523.6 50.4 %copy-start.19 = (f32[3,2,192,768]{3,2,1,0:T(8,128)S(1)}, f32[3,2,192,768]{3,2,1,0:T(8,128)}, u32[]{:S(2)}) copy-start(f32[3,2,192,768]{3,2,1,0:T(8,128)} %param.19) | copy-start | bytes 10616836
  (161 other events, 1375.1 us)
Sparse Core Ops, SparseCore 0:
  12.9 232.5 all-gather.22
  248.3 45.6 all-gather.24
  296.3 29.3 all-gather.26
  327.8 36.6 all-gather.28
  366.5 36.6 all-gather.30
  405.8 45.7 all-gather.32
  453.8 29.2 all-gather.34
  485.4 36.6 all-gather.36
  524.9 36.6 all-gather.38
  1117.1 47.0 reduce-scatter.37
  1169.2 65.4 all-reduce.35
  1238.6 48.8 reduce-scatter.35
  1291.8 60.4 reduce-scatter.23
  1356.5 60.4 reduce-scatter.21
  1421.6 97.2 reduce-scatter.17
  1524.2 97.2 reduce-scatter.19
  1626.0 79.4 reduce-scatter.31
  1710.1 79.4 reduce-scatter.29
  1794.2 79.4 reduce-scatter.25
  1878.3 79.4 reduce-scatter.27
  1963.1 546.7 reduce-scatter.33
where the time goes:
time: 2650 us; the launch traced here: 2630 us
  waiting for transfers between devices  1280 us (48%)
  matrix products  649 us (24%)
  other arithmetic  290 us (11%)
  local copies, waits for them, and re-layouts  287 us (11%)
  blocking collectives  97.8 us (4%)
    unnamed x25, waiting for transfers between devices  553 us
    reduce_scatter x8, waiting for transfers between devices, spread(): lax.psum_scatter(full.astype(jnp.float32), 'dp', scatter_dimension=axis,...  472 us
    all_gather x9, waiting for transfers between devices, collect(): lax.all_gather(local.astype(jnp.bfloat16), 'dp', axis=axis, tiled=True)  257 us
    dot_general x2, matrix products, row_step(): jnp.einsum('sv,sd->vd', d_logits, h_row, preferred_element_type=jnp.float32)  174 us
    unnamed x353, local copies, waits for them, and re-layouts  173 us
    dot_general x2, matrix products, row_step(): jnp.einsum('sd,vd->sv', h_row, head_w, preferred_element_type=jnp.float32)  108 us
    scatter-add x1, other arithmetic, train_step(): jax.ops.segment_sum(d_resid.reshape(-1, d_model), token_ids.reshape(-1),...  97.9 us
    dot_general x2, matrix products, row_step(): jnp.einsum('sv,vd->sd', d_logits, head_w, preferred_element_type=jnp.floa...  86.3 us
  transfers between devices with their start and end apart: 21, of which 12 were waited for; matrix products, arithmetic and copies ran while one was open for 22% of the time, Pallas kernels for 0%

commit v1 on v0

v1 whole, which is shorter than its diff:
```python
import functools

import jax
import jax.numpy as jnp
from jax import lax
from jax.experimental import pallas as pl
from jax.experimental.pallas import tpu as pltpu
from jax.sharding import PartitionSpec as P

NORM_EPS = 1e-5
LEARN_RATE = 3e-3
BETA_ONE = 0.9
BETA_TWO = 0.95
ADAM_EPS = 1e-8
WEIGHT_DECAY = 0.1
CLIP_NORM = 1.0
ADAM_STEP = 10
DECAYS = (WEIGHT_DECAY,) * 6 + (0.0, 0.0)
LANES = 128
TOKEN_TILE = 512
VOCAB_TILE = 512
VMEM_BYTES = 60 * 1024 * 1024


def layer_norm(residual, gain, bias):
    mean_val = jnp.mean(residual, axis=-1, keepdims=True)
    centered = residual - mean_val
    variance = jnp.mean(centered * centered, axis=-1, keepdims=True)
    return centered * lax.rsqrt(variance + NORM_EPS) * gain.astype(jnp.float32) + bias.astype(jnp.float32)


def attention_half(residual, qkv_w, proj_t, layer_vec, num_heads, ff_dim):
    batch, seq_len, d_model = residual.shape
    head_dim = d_model // num_heads
    offset = 4 * d_model + ff_dim
    ln_par = layer_vec[offset + d_model:].reshape(4, d_model)
    normed_in = layer_norm(residual, ln_par[0], ln_par[1]).astype(jnp.bfloat16)
    qkv_all = jnp.einsum('bsd,tde->tbse', normed_in, qkv_w, preferred_element_type=jnp.float32)
    qkv_all = (qkv_all + layer_vec[:3 * d_model].astype(jnp.float32).reshape(3, 1, 1, d_model)).astype(jnp.bfloat16)
    qkv_all = qkv_all.reshape(3, batch, seq_len, num_heads, head_dim)
    scores = jnp.einsum('bqhk,bshk->bhqs', qkv_all[0], qkv_all[1], preferred_element_type=jnp.float32) * head_dim ** -0.5
    rows_iota = lax.broadcasted_iota(jnp.int32, (seq_len, seq_len), 0)
    cols_iota = lax.broadcasted_iota(jnp.int32, (seq_len, seq_len), 1)
    scores = jnp.where(rows_iota >= cols_iota, scores, -1e30)
    attn_prob = jax.nn.softmax(scores, axis=-1).astype(jnp.bfloat16)
    mixed = jnp.einsum('bhqs,bshk->bqhk', attn_prob, qkv_all[2], preferred_element_type=jnp.float32).astype(jnp.bfloat16)
    mixed = mixed.reshape(batch, seq_len, d_model)
    return residual + jnp.einsum('bsl,el->bse', mixed, proj_t, preferred_element_type=jnp.float32) + layer_vec[3 * d_model:4 * d_model].astype(jnp.float32)


def feed_half(residual, up_w, down_w, layer_vec):
    d_model, ff_dim = up_w.shape
    offset = 4 * d_model + ff_dim
    ln_par = layer_vec[offset + d_model:].reshape(4, d_model)
    normed_mid = layer_norm(residual, ln_par[2], ln_par[3]).astype(jnp.bfloat16)
    hidden = jax.nn.relu(jnp.einsum('bsd,df->bsf', normed_mid, up_w, preferred_element_type=jnp.float32) + layer_vec[4 * d_model:offset].astype(jnp.float32)).astype(jnp.bfloat16)
    return residual + jnp.einsum('bsf,fd->bsd', hidden, down_w, preferred_element_type=jnp.float32) + layer_vec[offset:offset + d_model].astype(jnp.float32)


def final_norm(residual, lnf_c):
    return layer_norm(residual, lnf_c[0], lnf_c[1]).astype(jnp.bfloat16)


def lookup_kernel(ids_ref, table_ref, out_ref):
    def step(i, carry):
        base = pl.multiple_of(i * 8, 8)
        rows = [table_ref[pl.ds(ids_ref[base + u], 1), :] for u in range(8)]
        out_ref[pl.ds(base, 8), :] = jnp.concatenate(rows, axis=0)
        return carry

    lax.fori_loop(0, out_ref.shape[0] // 8, step, 0)


def lookup_rows(ids, table):
    count = ids.shape[0]
    return pl.pallas_call(
        lookup_kernel,
        out_shape=jax.ShapeDtypeStruct((count, LANES), jnp.float32),
        in_specs=[pl.BlockSpec(memory_space=pltpu.SMEM), pl.BlockSpec(memory_space=pltpu.VMEM)],
        out_specs=pl.BlockSpec(memory_space=pltpu.VMEM),
        compiler_params=pltpu.CompilerParams(vmem_limit_bytes=VMEM_BYTES),
        cost_estimate=pl.CostEstimate(flops=10 ** 10, bytes_accessed=count * 2 * LANES * 4 + table.size * 4, transcendentals=0),
    )(ids, table)


def accumulate_kernel(ids_ref, rows_ref, acc_ref):
    def clear(i, carry):
        acc_ref[pl.ds(pl.multiple_of(i * 512, 512), 512), :] = jnp.zeros((512, LANES), jnp.float32)
        return carry

    lax.fori_loop(0, acc_ref.shape[0] // 512, clear, 0)

    def step(i, carry):
        base = pl.multiple_of(i * 8, 8)
        rows = rows_ref[pl.ds(base, 8), :]
        for u in range(8):
            idx = ids_ref[base + u]
            acc_ref[pl.ds(idx, 1), :] = acc_ref[pl.ds(idx, 1), :] + rows[u:u + 1, :]
        return carry

    lax.fori_loop(0, rows_ref.shape[0] // 8, step, 0)


def accumulate_rows(ids, rows, num_rows):
    return pl.pallas_call(
        accumulate_kernel,
        out_shape=jax.ShapeDtypeStruct((num_rows, LANES), jnp.float32),
        in_specs=[pl.BlockSpec(memory_space=pltpu.SMEM), pl.BlockSpec(memory_space=pltpu.VMEM)],
        out_specs=pl.BlockSpec(memory_space=pltpu.VMEM),
        compiler_params=pltpu.CompilerParams(vmem_limit_bytes=VMEM_BYTES),
        cost_estimate=pl.CostEstimate(flops=10 ** 10, bytes_accessed=rows.size * 4 + num_rows * LANES * 4, transcendentals=0),
    )(ids, rows)


def head_forward_kernel(h_ref, head_ref, mask_ref, u_ref, lse_ref, logit_ref):
    h_tile = h_ref[...]
    slice_len = head_ref.shape[1]
    top = jnp.full((h_tile.shape[0], 1), -jnp.inf, jnp.float32)
    for start in range(0, slice_len, VOCAB_TILE):
        cols = slice(start, start + VOCAB_TILE)
        logits = jnp.dot(h_tile, head_ref[:, cols], preferred_element_type=jnp.float32) + mask_ref[:, cols]
        logit_ref[:, cols] = logits
        top = jnp.maximum(top, jnp.max(logits, axis=-1, keepdims=True))
    total = jnp.zeros_like(top)
    for start in range(0, slice_len, VOCAB_TILE):
        cols = slice(start, start + VOCAB_TILE)
        exp_shift = jnp.exp(logit_ref[:, cols] - top)
        total = total + jnp.sum(exp_shift, axis=-1, keepdims=True)
        part = lax.dot_general(exp_shift.astype(jnp.bfloat16), head_ref[:, cols], (((1,), (1,)), ((), ())), preferred_element_type=jnp.float32)
        if start == 0:
            u_ref[...] = part
        else:
            u_ref[...] += part
    u_ref[...] = u_ref[...] * (1.0 / total)
    lse_ref[...] = top + jnp.log(total)


def head_forward(h_all, head_t, mask):
    tokens, d_model = h_all.shape
    slice_len = head_t.shape[1]
    return pl.pallas_call(
        head_forward_kernel,
        grid=(tokens // TOKEN_TILE,),
        out_shape=(jax.ShapeDtypeStruct((tokens, d_model), jnp.float32), jax.ShapeDtypeStruct((tokens, 1), jnp.float32)),
        in_specs=[pl.BlockSpec((TOKEN_TILE, d_model), lambda i: (i, 0)), pl.BlockSpec((d_model, slice_len), lambda i: (0, 0)), pl.BlockSpec((1, slice_len), lambda i: (0, 0))],
        out_specs=(pl.BlockSpec((TOKEN_TILE, d_model), lambda i: (i, 0)), pl.BlockSpec((TOKEN_TILE, 1), lambda i: (i, 0))),
        scratch_shapes=[pltpu.VMEM((TOKEN_TILE, slice_len), jnp.float32)],
        compiler_params=pltpu.CompilerParams(vmem_limit_bytes=VMEM_BYTES, dimension_semantics=('arbitrary',)),
        cost_estimate=pl.CostEstimate(flops=4 * tokens * d_model * slice_len, bytes_accessed=tokens * d_model * 6 + head_t.size * 2, transcendentals=tokens * slice_len),
    )(h_all, head_t, mask)


def head_grad_kernel(inv_tokens, h_ref, head_ref, mask_ref, lse_ref, tgt_ref, grad_ref, flip_ref):
    h_tile = h_ref[...]
    slice_len = head_ref.shape[1]
    flip_ref[...] = jnp.transpose(h_tile)
    lse = lse_ref[...]
    tgt = tgt_ref[...]

    @pl.when(pl.program_id(0) == 0)
    def _():
        grad_ref[...] = jnp.zeros_like(grad_ref)

    for start in range(0, slice_len, VOCAB_TILE):
        cols = slice(start, start + VOCAB_TILE)
        logits = jnp.dot(h_tile, head_ref[:, cols], preferred_element_type=jnp.float32) + mask_ref[:, cols]
        prob = jnp.exp(logits - lse) * inv_tokens
        is_target = lax.broadcasted_iota(jnp.int32, logits.shape, 1) == tgt - start
        d_logits = jnp.where(is_target, prob - inv_tokens, prob).astype(jnp.bfloat16)
        grad_ref[:, cols] += jnp.dot(flip_ref[...], d_logits, preferred_element_type=jnp.float32)


def head_grad(h_all, head_t, mask, lse, tgt, inv_tokens):
    tokens, d_model = h_all.shape
    slice_len = head_t.shape[1]
    return pl.pallas_call(
        functools.partial(head_grad_kernel, inv_tokens),
        grid=(tokens // TOKEN_TILE,),
        out_shape=jax.ShapeDtypeStruct((d_model, slice_len), jnp.float32),
        in_specs=[pl.BlockSpec((TOKEN_TILE, d_model), lambda i: (i, 0)), pl.BlockSpec((d_model, slice_len), lambda i: (0, 0)), pl.BlockSpec((1, slice_len), lambda i: (0, 0)), pl.BlockSpec((TOKEN_TILE, 1), lambda i: (i, 0)), pl.BlockSpec((TOKEN_TILE, 1), lambda i: (i, 0))],
        out_specs=pl.BlockSpec((d_model, slice_len), lambda i: (0, 0)),
        scratch_shapes=[pltpu.VMEM((d_model, TOKEN_TILE), jnp.bfloat16)],
        compiler_params=pltpu.CompilerParams(vmem_limit_bytes=VMEM_BYTES, dimension_semantics=('arbitrary',)),
        cost_estimate=pl.CostEstimate(flops=4 * tokens * d_model * slice_len, bytes_accessed=tokens * d_model * 2 + head_t.size * 6, transcendentals=tokens * slice_len),
    )(h_all, head_t, mask, lse, tgt)


def adam_update(state, grad, decay):
    moment = BETA_ONE * state[1] + (1.0 - BETA_ONE) * grad
    second = BETA_TWO * state[2] + (1.0 - BETA_TWO) * grad * grad
    m_hat = moment / (1.0 - BETA_ONE ** ADAM_STEP)
    v_hat = second / (1.0 - BETA_TWO ** ADAM_STEP)
    master = state[0] * (1.0 - LEARN_RATE * decay) - LEARN_RATE * m_hat / (jnp.sqrt(v_hat) + ADAM_EPS)
    return jnp.stack([master, moment, second])


def solution(mesh):
    n_dev = mesh.shape['dp']
    row_spec = P('dp', None)
    state_specs = (P(None, None, 'dp'), P(None, None, 'dp'), P(None, None, 'dp', None, None, None), P(None, None, None, None, 'dp'), P(None, None, 'dp', None), P(None, None, 'dp', None), P(None, None, 'dp'), P(None, None, 'dp'))

    def gather(local):
        return lax.all_gather(local, 'dp', axis=0, tiled=False)

    def scatter_sum(full):
        return lax.psum_scatter(full, 'dp', scatter_dimension=0, tiled=False)

    def swap(blocks):
        return lax.all_to_all(blocks, 'dp', split_axis=0, concat_axis=0, tiled=False)

    def train_step(token_ids, target_ids, st_wte, st_wpe, st_qkv, st_proj, st_up, st_down, st_vec, st_lnf):
        num_layers, shard = st_qkv.shape[1], st_qkv.shape[2]
        num_heads = st_qkv.shape[4]
        batch_dev, seq_len = token_ids.shape
        vocab_size = st_wte.shape[1]
        pos_rows = st_wpe.shape[1]
        d_model = shard * n_dev
        ff_shard = st_down.shape[2]
        ff_dim = ff_shard * n_dev
        ff_parts = ff_dim // d_model
        vec_shard = st_vec.shape[2]
        tok_dev = batch_dev * seq_len
        tokens = tok_dev * n_dev
        inv_tokens = 1.0 / tokens
        slice_len = -(-vocab_size // (n_dev * VOCAB_TILE)) * VOCAB_TILE
        vocab_pad = slice_len * n_dev
        me = lax.axis_index('dp')

        def pack_attn(qkv, proj):
            return [jnp.swapaxes(qkv.reshape(shard, 3, d_model), 0, 1).reshape(3 * shard, d_model), proj.reshape(d_model, shard).T]

        def pack_feed(up, down):
            return [jnp.swapaxes(up.reshape(shard, ff_parts, d_model), 0, 1).reshape(ff_parts * shard, d_model), down]

        pos_pack = st_wpe[0, 2:2 + seq_len].T.reshape(-1, d_model)
        pos_count = pos_pack.shape[0]
        small_rows = jnp.concatenate([st_vec[0], jnp.pad(st_lnf[0].reshape(1, -1), ((0, 0), (0, vec_shard - 2 * shard)))], axis=0)
        small_rows = jnp.pad(small_rows, ((0, (-(num_layers + 1 + pos_count)) % 16), (0, d_model - vec_shard)))

        def half_pack(parts):
            return jnp.concatenate([part.astype(jnp.bfloat16) for part in parts], axis=0)

        gathered_attn, gathered_feed = [], []
        for layer in range(num_layers):
            parts = pack_attn(st_qkv[0, layer], st_proj[0, layer])
            if layer == 0:
                parts = parts + [pos_pack, small_rows]
            gathered_attn.append(gather(half_pack(parts)))
            gathered_feed.append(gather(half_pack(pack_feed(st_up[0, layer], st_down[0, layer]))))

        ids_all = lax.all_gather(jnp.stack([token_ids, target_ids]), 'dp', axis=1, tiled=True).reshape(2, tokens)
        table = jnp.pad(st_wte[0], ((0, 0), (0, LANES - shard)))

        def spread_rows(rows):
            cols = rows[:, :shard].astype(jnp.bfloat16).T.reshape(shard, n_dev, tok_dev)
            return swap(jnp.swapaxes(cols, 0, 1)).reshape(d_model, tok_dev).T

        token_rows = spread_rows(lookup_rows(ids_all[0], table))

        attn_rows = 4 * shard
        first = gathered_attn[0]
        pos_c = first[:, attn_rows:attn_rows + pos_count].reshape(d_model, seq_len).T
        small_c = first[:, attn_rows + pos_count:attn_rows + pos_count + num_layers + 1, :vec_shard]
        vec_c = [small_c[:, layer].reshape(-1) for layer in range(num_layers)]
        lnf_c = jnp.swapaxes(small_c[:, num_layers, :2 * shard].reshape(n_dev, 2, shard), 0, 1).reshape(2, d_model)

        def attn_weights(block):
            qkv_w = jnp.swapaxes(block[:, :3 * shard].reshape(n_dev, 3, shard, d_model), 0, 1).reshape(3, d_model, d_model)
            return qkv_w, block[:, 3 * shard:attn_rows].reshape(d_model, d_model)

        def feed_weights(block):
            up_w = jnp.swapaxes(block[:, :ff_parts * shard].reshape(n_dev, ff_parts, shard, d_model), 1, 2).reshape(d_model, ff_dim)
            return up_w, block[:, ff_parts * shard:].reshape(ff_dim, d_model)

        residual = token_rows.astype(jnp.float32).reshape(batch_dev, seq_len, d_model) + pos_c.astype(jnp.float32)
        attn_backs, feed_backs = [], []
        for layer in range(num_layers):
            qkv_w, proj_t = attn_weights(gathered_attn[layer])
            residual, back = jax.vjp(lambda x, a, b, c: attention_half(x, a, b, c, num_heads, ff_dim), residual, qkv_w, proj_t, vec_c[layer])
            attn_backs.append(back)
            up_w, down_w = feed_weights(gathered_feed[layer])
            residual, back = jax.vjp(feed_half, residual, up_w, down_w, vec_c[layer])
            feed_backs.append(back)
        normed, norm_back = jax.vjp(final_norm, residual, lnf_c)

        head_send = jnp.pad(st_wte[0].T.astype(jnp.bfloat16), ((0, 0), (0, vocab_pad - vocab_size)))
        head_send = jnp.swapaxes(head_send.reshape(shard, n_dev, slice_len), 0, 1)
        head_t = swap(head_send).reshape(d_model, slice_len)
        vocab_pos = me * slice_len + lax.broadcasted_iota(jnp.int32, (1, slice_len), 1)
        mask = jnp.where(vocab_pos < vocab_size, 0.0, -1e30).astype(jnp.float32)
        tgt_local = (ids_all[1] - me * slice_len).reshape(n_dev, batch_dev, seq_len)

        h_alls = [gather(normed[row]).reshape(n_dev * seq_len, d_model) for row in range(batch_dev)]
        late_ids, _ = lax.optimization_barrier((ids_all[1], normed))
        target_rows = spread_rows(lookup_rows(late_ids, table)).astype(jnp.float32).reshape(batch_dev, seq_len, d_model)
        lse_alls, d_parts, loss_part = [], [], 0.0
        for row in range(batch_dev):
            u_part, lse_part = head_forward(h_alls[row], head_t, mask)
            lse_dev = lax.all_gather(lse_part.reshape(-1), 'dp', axis=0, tiled=False)
            top = jnp.max(lse_dev, axis=0)
            lse = top + jnp.log(jnp.sum(jnp.exp(lse_dev - top), axis=0))
            factor = jnp.exp(lse_part - lse[:, None]) * inv_tokens
            d_sum = scatter_sum((u_part * factor).reshape(n_dev, seq_len, d_model))
            d_parts.append(d_sum - inv_tokens * target_rows[row])
            lse_alls.append(lse[:, None])
            own = lax.dynamic_slice_in_dim(lse, me * seq_len, seq_len)
            picked = jnp.sum(normed[row].astype(jnp.float32) * target_rows[row], axis=-1)
            loss_part = loss_part + jnp.sum(own - picked) * inv_tokens
        d_normed = jnp.stack(d_parts)
        head_parts = [head_grad(h_alls[row], head_t, mask, lse_alls[row], tgt_local[:, row].reshape(-1, 1), inv_tokens) for row in range(batch_dev)]
        grad_head = functools.reduce(jnp.add, head_parts)
        grad_head = swap(grad_head.reshape(n_dev, shard, slice_len))
        grad_head = jnp.swapaxes(grad_head, 0, 1).reshape(shard, vocab_pad)[:, :vocab_size].T

        d_resid, d_lnf = norm_back(d_normed.astype(jnp.bfloat16))
        d_vec = [None] * num_layers
        qkv_g, proj_g, up_g, down_g = ([None] * num_layers for _ in range(4))
        small_g = None
        for layer in reversed(range(num_layers)):
            d_resid, d_up, d_down, d_vec_b = feed_backs[layer](d_resid)
            up_rows = jnp.swapaxes(d_up.reshape(n_dev, shard, ff_parts, d_model), 1, 2).reshape(n_dev, ff_parts * shard, d_model)
            summed = scatter_sum(jnp.concatenate([up_rows, d_down.reshape(n_dev, ff_shard, d_model)], axis=1).astype(jnp.float32))
            up_g[layer] = jnp.swapaxes(summed[:ff_parts * shard].reshape(ff_parts, shard, d_model), 0, 1).reshape(shard, ff_dim)
            down_g[layer] = summed[ff_parts * shard:]
            d_resid, d_qkv, d_proj, d_vec_a = attn_backs[layer](d_resid)
            d_vec[layer] = d_vec_a + d_vec_b
            qkv_rows = jnp.swapaxes(d_qkv.reshape(3, n_dev, shard, d_model), 0, 1).reshape(n_dev, 3 * shard, d_model)
            parts = [qkv_rows.astype(jnp.float32), d_proj.reshape(n_dev, shard, d_model).astype(jnp.float32)]
            if layer == 0:
                pos_sum = jnp.sum(d_resid, axis=0).T.reshape(n_dev, pos_count, d_model)
                rows = [vec.astype(jnp.float32).reshape(n_dev, 1, vec_shard) for vec in d_vec]
                rows.append(jnp.pad(jnp.swapaxes(d_lnf.astype(jnp.float32).reshape(2, n_dev, shard), 0, 1).reshape(n_dev, 1, 2 * shard), ((0, 0), (0, 0), (0, vec_shard - 2 * shard))))
                rows = jnp.concatenate(rows, axis=1)
                rows = jnp.pad(rows, ((0, 0), (0, (-(num_layers + 1 + pos_count)) % 8), (0, d_model - vec_shard)))
                parts = parts + [pos_sum, rows]
            summed = scatter_sum(jnp.concatenate(parts, axis=1))
            qkv_g[layer] = jnp.swapaxes(summed[:3 * shard].reshape(3, shard, d_model), 0, 1).reshape(st_qkv.shape[2:])
            proj_g[layer] = summed[3 * shard:attn_rows].T.reshape(st_proj.shape[2:])
            if layer == 0:
                pos_g = jnp.pad(summed[attn_rows:attn_rows + pos_count].reshape(shard, seq_len).T, ((2, pos_rows - 2 - seq_len), (0, 0)))
                small_g = summed[attn_rows + pos_count:attn_rows + pos_count + num_layers + 1, :vec_shard]
        vec_g = small_g[:num_layers]
        lnf_g = small_g[num_layers, :2 * shard].reshape(2, shard)

        lookup_d = swap(d_resid.reshape(tok_dev, d_model).T.reshape(n_dev, shard, tok_dev))
        lookup_d = jnp.pad(jnp.swapaxes(lookup_d, 1, 2).reshape(tokens, shard), ((0, 0), (0, LANES - shard)))
        wte_g = grad_head + accumulate_rows(ids_all[0], lookup_d, vocab_pad)[:vocab_size, :shard]

        grads = [wte_g, pos_g, jnp.stack(qkv_g), jnp.stack(proj_g), jnp.stack(up_g), jnp.stack(down_g), vec_g, lnf_g]
        local_sq = sum(jnp.sum(grad * grad) for grad in grads)
        sums = lax.psum(jnp.stack([local_sq, loss_part]), 'dp')
        clip_coef = jnp.minimum(1.0, CLIP_NORM / (jnp.sqrt(sums[0]) + 1e-6))
        states = (st_wte, st_wpe, st_qkv, st_proj, st_up, st_down, st_vec, st_lnf)
        new_states = tuple(adam_update(state, grad * clip_coef, decay) for state, grad, decay in zip(states, grads, DECAYS))
        return (sums[1],) + new_states

    return jax.shard_map(train_step, mesh=mesh, in_specs=(row_spec, row_spec) + state_specs, out_specs=(P(),) + state_specs, check_vma=False)
```

time: 2650 us -> 2100 us (0.79)
  waiting for transfers between devices: 1280 us -> 293 us
  matrix products: 649 us -> 229 us
  Pallas kernels: 0 us -> 401 us
  blocking collectives: 97.8 us -> 422 us
  local copies, waits for them, and re-layouts: 287 us -> 365 us
  other arithmetic: 290 us -> 342 us
    unnamed x25 -> x12, waiting for transfers between devices: 553 us -> 0.7 us
    dot_general x40 -> x34, matrix products: 630 us -> 210 us  [the longest x6 49.3 us: feed_half(): jnp.einsum('bsd,df->bsf', normed_mid, up_w, preferred_element_type=jnp.fl...]
    reduce_scatter x8 -> x6, waiting for transfers between devices: 472 us -> 54.9 us  [scatter_sum(): return lax.psum_scatter(full, 'dp', scatter_dimension=0, tiled=False)]
    pallas_call x0 -> x7, Pallas kernels: none -> 401 us  [the longest x2 153 us: head_forward(): pl.pallas_call(head_forward_kernel, grid=(tokens // TOKEN_TILE,), out_sha...]
    all_gather x2 -> x3, blocking collectives: 29.3 us -> 388 us  [the longest x2 373 us: train_step(): lse_dev = lax.all_gather(lse_part.reshape(-1), 'dp', axis=0, tiled=False)]
    all_gather x9 -> x6, waiting for transfers between devices: 257 us -> 0.06 us  [gather(): return lax.all_gather(local, 'dp', axis=0, tiled=False)]
    all_to_all x0 -> x5, waiting for transfers between devices: none -> 237 us  [swap(): lax.all_to_all(blocks, 'dp', split_axis=0, concat_axis=0, tiled=False)]
    unnamed x353 -> x373, local copies, waits for them, and re-layouts: 173 us -> 64.5 us
  transfers between devices with their start and end apart: 21 -> 17, of which waited for: 12 -> 5; matrix products, arithmetic and copies ran while one was open for 22% -> 30% of each run, Pallas kernels for 0% -> 19%
where the time goes in v1:
time: 2100 us; the launch traced here: 2090 us
  blocking collectives  422 us (20%)
  Pallas kernels  401 us (19%)
  local copies, waits for them, and re-layouts  365 us (17%)
  other arithmetic  342 us (16%)
  waiting for transfers between devices  293 us (14%)
  matrix products  229 us (11%)
  between operations  24 us (1%)
    all_gather x2, blocking collectives, train_step(): lse_dev = lax.all_gather(lse_part.reshape(-1), 'dp', axis=0, tiled=False)  373 us
    all_to_all x5, waiting for transfers between devices, swap(): lax.all_to_all(blocks, 'dp', split_axis=0, concat_axis=0, tiled=False)  237 us
    pallas_call x2, Pallas kernels, head_forward(): pl.pallas_call(head_forward_kernel, grid=(tokens // TOKEN_TILE,), out_sha...  153 us
    pallas_call x2, Pallas kernels, head_grad(): pl.pallas_call(functools.partial(head_grad_kernel, inv_tokens), grid=(tok...  148 us
    another operation x11, other arithmetic, adam_update(): return jnp.stack([master, moment, second])  71.2 us
    unnamed x373, local copies, waits for them, and re-layouts  64.5 us
    reduce_scatter x6, waiting for transfers between devices, scatter_sum(): return lax.psum_scatter(full, 'dp', scatter_dimension=0, tiled=False)  54.9 us
    pallas_call x2, Pallas kernels, lookup_rows(): pl.pallas_call(lookup_kernel, out_shape=jax.ShapeDtypeStruct((count, LANE...  54.6 us
  transfers between devices with their start and end apart: 17, of which 5 were waited for; matrix products, arithmetic and copies ran while one was open for 30% of the time, Pallas kernels for 19%

profile of v1, /device:TPU:0, one launch (start us, length us, event | category | flops | bytes accessed | tf_op | source)
XLA Modules:
  0.0 2091.6 jit_solution(17342234426025977350)
XLA Ops:
  24.7 16.6 fusion.172
  41.3 13.8 copy.329
  55.2 16.6 pad.122.table_ref
  71.8 15.2 all_gather.39
  88.3 27.3 %shard_map.169 = f32[12288,128]{1,0:T(8,128)} custom-call(s32[12288]{0:T(1024)} %bitcast.589, f32[40478,128]{1,0:T(8,128)} %pad.122.table_ref), custom_call_target="tpu_custom_call" | custom-call | flops 10000000000 | bytes 33307648 | tf_op jit(solution)/shard_map/pallas_call | solution.py:76
  124.4 25.8 %all-to-all-done = bf16[16,48,768]{2,1,0:T(8,128)(2,1)S(1)} async-done(((bf16[16,48,768]{2,1,0:T(8,128)(2,1)}), bf16[16,48,768]{2,1,0:T(8,128)(2,1)S(1)}, u32[]{:S(2)}, u32[]{:S(2)}) %all-to-all-start) | async-done | bytes 1179680 | tf_op jit(solution)/shard_map/all_to_all | solution.py:209
  360.1 63.1 %all-to-all-done.1 = bf16[16,48,2560]{2,1,0:T(8,128)(2,1)} async-done(((bf16[16,48,2560]{2,1,0:T(8,128)(2,1)}), bf16[16,48,2560]{2,1,0:T(8,128)(2,1)}, u32[]{:S(2)}, u32[]{:S(2)}) %all-to-all-start.1) | async-done | bytes 3932192 | tf_op jit(solution)/shard_map/all_to_all | solution.py:209
  423.2 76.4 %shard_map.170 = (f32[6144,768]{1,0:T(8,128)}, f32[6144,1]{1,0:T(8,128)}) custom-call(bf16[6144,768]{1,0:T(8,128)(2,1)} %bitcast.594, bf16[768,2560]{1,0:T(8,128)(2,1)} %bitcast.72.head_ref, f32[1,2560]{1,0:T(1,128)} %compare_select_fusion.mask_ref), custom_call_target="tpu_custom_call" | custom-call | flops 48318382080 | bytes 32243712 | tf_op jit(solution)/shard_map/pallas_call | solution.py:141
  499.7 179.0 %all-gather.4 = f32[98304,1]{1,0:T(8,128)} all-gather(f32[6144,1]{1,0:T(8,128)} %get-tuple-element.14), channel_id=6, replica_groups=mesh['dp'=16] {'dp'}, dimensions={0}, use_global_device_ids=true | all-gather | bytes 417792 | tf_op jit(solution)/shard_map/all_gather | solution.py:299
  678.7 23.0 %reduce.23 = f32[98304]{0:T(1024)} reduce(f32[98304,1]{1,0:T(8,128)} %all-gather.4, f32[]{:T(128)} %constant.264), dimensions={1}, to_apply=%all-gather.4.reduce_sub_computation | reduce | bytes 786436 | tf_op jit(solution)/shard_map/all_gather | solution.py:299
  710.2 15.4 broadcast_multiply_fusion.1
  725.7 76.6 %shard_map.172 = (f32[6144,768]{1,0:T(8,128)}, f32[6144,1]{1,0:T(8,128)}) custom-call(bf16[6144,768]{1,0:T(8,128)(2,1)} %bitcast.596, bf16[768,2560]{1,0:T(8,128)(2,1)} %bitcast.72.head_ref, f32[1,2560]{1,0:T(1,128)} %compare_select_fusion.mask_ref), custom_call_target="tpu_custom_call" | custom-call | flops 48318382080 | bytes 32243712 | tf_op jit(solution)/shard_map/pallas_call | solution.py:141
  802.3 193.9 %all-gather.5 = f32[98304,1]{1,0:T(8,128)} all-gather(f32[6144,1]{1,0:T(8,128)} %get-tuple-element.15), channel_id=7, replica_groups=mesh['dp'=16] {'dp'}, dimensions={0}, use_global_device_ids=true | all-gather | bytes 417792 | tf_op jit(solution)/shard_map/all_gather | solution.py:299
  996.2 23.0 %reduce.25 = f32[98304]{0:T(1024)} reduce(f32[98304,1]{1,0:T(8,128)} %all-gather.5, f32[]{:T(128)} %constant.264), dimensions={1}, to_apply=%all-gather.5.reduce_sub_computation | reduce | bytes 786436 | tf_op jit(solution)/shard_map/all_gather | solution.py:299
  1027.8 15.3 broadcast_multiply_fusion
  1045.5 27.3 %shard_map.174 = f32[12288,128]{1,0:T(8,128)} custom-call(s32[12288]{0:T(1024)} %bitcast.591, f32[40478,128]{1,0:T(8,128)} %pad.122.table_ref), custom_call_target="tpu_custom_call" | custom-call | flops 10000000000 | bytes 33307648 | tf_op jit(solution)/shard_map/pallas_call | solution.py:76
  1088.5 22.6 %all-to-all-done.3 = bf16[16,48,768]{2,1,0:T(8,128)(2,1)S(1)} async-done(((bf16[16,48,768]{2,1,0:T(8,128)(2,1)}), bf16[16,48,768]{2,1,0:T(8,128)(2,1)S(1)}, u32[]{:S(2)}, u32[]{:S(2)}) %all-to-all-start.3) | async-done | bytes 1179680 | tf_op jit(solution)/shard_map/all_to_all | solution.py:209
  1115.2 54.9 %reduce-scatter.9.cloned.1.call-done = f32[1,384,768]{2,1,0:T(8,128)} async-done(((f32[16,384,768]{2,1,0:T(8,128)}), f32[1,384,768]{2,1,0:T(8,128)}) %reduce-scatter.9.cloned.1.call-update) | async-done | bytes 1179664 | tf_op jit(solution)/shard_map/reduce_scatter | solution.py:206
  1462.4 73.9 %shard_map.171 = f32[768,2560]{1,0:T(8,128)} custom-call(bf16[6144,768]{1,0:T(8,128)(2,1)} %bitcast.595, bf16[768,2560]{1,0:T(8,128)(2,1)} %bitcast.72.head_ref, f32[1,2560]{1,0:T(1,128)} %compare_select_fusion.mask_ref, f32[6144,1]{1,0:T(8,128)} %copy.239.lse_ref, s32[6144,1]{1,0:T(8,128)} %copy.340.tgt_ref), custom_call_target="tpu_custom_call" | custom-call | flops 48318382080 | bytes 21233664 | tf_op jit(solution)/shard_map/pallas_call | solution.py:176
  1536.4 74.0 %shard_map.173 = f32[768,2560]{1,0:T(8,128)} custom-call(bf16[6144,768]{1,0:T(8,128)(2,1)} %bitcast.597, bf16[768,2560]{1,0:T(8,128)(2,1)} %bitcast.72.head_ref, f32[1,2560]{1,0:T(1,128)} %compare_select_fusion.mask_ref, f32[6144,1]{1,0:T(8,128)} %copy.242.lse_ref, s32[6144,1]{1,0:T(8,128)} %copy.341.tgt_ref), custom_call_target="tpu_custom_call" | custom-call | flops 48318382080 | bytes 21233664 | tf_op jit(solution)/shard_map/pallas_call | solution.py:176
  1626.3 125.6 %all-to-all-done.2 = f32[16,48,2560]{2,1,0:T(8,128)} async-done(((f32[16,48,2560]{2,1,0:T(8,128)}), f32[16,48,2560]{2,1,0:T(8,128)}, u32[]{:S(2)}, u32[]{:S(2)}) %all-to-all-start.2) | async-done | bytes 7864352 | tf_op jit(solution)/shard_map/all_to_all | solution.py:209
  1755.0 13.8 copy.332
  1768.9 13.8 copy.333
  1793.6 14.0 copy.244
  1816.4 45.8 %shard_map.175 = f32[40960,128]{1,0:T(8,128)} custom-call(s32[12288]{0:T(1024)} %bitcast.590, f32[12288,128]{1,0:T(8,128)} %pad.132.rows_ref), custom_call_target="tpu_custom_call" | custom-call | flops 10000000000 | bytes 27262976 | tf_op jit(solution)/shard_map/pallas_call | solution.py:105
  1862.1 22.4 %multiply_reduce_fusion = (f32[]{:T(128)}, f32[40478,48]{1,0:T(8,128)}) fusion(f32[40960,128]{1,0:T(8,128)} %shard_map.175, f32[48,40960]{0,1:T(8,128)} %bitcast.448), kind=kLoop, calls=%fused_computation.9 | loop fusion | flops 5828831 | bytes 23315332 | tf_op jit(solution)/shard_map/reduce_sum | solution.py:350
  1914.2 33.6 %psum.7 = f32[2]{0:T(128)S(1)} all-reduce(f32[2]{0:T(128)S(1)} %pad_maximum_fusion.13), channel_id=1, replica_groups=mesh['dp'=16] {'dp'}, use_global_device_ids=true, to_apply=%region_68.69 | all-reduce | flops 2 | bytes 16 | tf_op jit(solution)/shard_map/psum | solution.py:351
  1952.2 46.6 %subtract_bitcast_fusion = (f32[1,40478,48]{2,1,0:T(8,128)}, f32[1,40478,48]{2,1,0:T(8,128)}, f32[1,40478,48]{2,1,0:T(8,128)}) fusion(f32[40478,48]{1,0:T(8,128)} %get-tuple-element.105, f32[]{:T(128)} %bitcast.183, f32[1,40478,48]{2,1,0:T(8,128)} %copy.332, f32[1,40478,48]{2,1,0:T(8,128)} %copy.333, f32[1,40478,48]{2,1,0:T(8,128)} %copy.329), kind=kLoop, calls=%fused_computation.8 | loop fusion | flops 27201216 | bytes 54402436 | tf_op jit(solution)/shard_map/stack | solution.py:194
  1998.8 14.7 copy.284
  2013.5 14.7 copy.283
  2028.3 14.9 copy.282
  2063.5 14.8 pad_maximum_fusion
  (715 shorter events, 658.8 us)
Async XLA Ops:
  7.2 145.3 %all-gather.21.cloned.1.call-start = ((), (), s32[]{:S(2)}) async-start(), calls=%async_computation.21 | async-start | bytes 5013504 | tf_op jit(solution)/shard_map/all_gather | solution.py:203
  13.4 145.7 %all-gather.17.cloned.1.call-start = ((), (), s32[]{:S(2)}) async-start(), calls=%async_computation.19 | async-start | bytes 5849088 | tf_op jit(solution)/shard_map/all_gather | solution.py:203
  17.4 204.8 %all-gather.19.cloned.1.call-start = ((), (), s32[]{:S(2)}) async-start(), calls=%async_computation.20 | async-start | bytes 10027008 | tf_op jit(solution)/shard_map/all_gather | solution.py:203
  23.5 244.9 %all-gather.23.cloned.1.call-start = ((), (), s32[]{:S(2)}) async-start(), calls=%async_computation.22 | async-start | bytes 10027008 | tf_op jit(solution)/shard_map/all_gather | solution.py:203
  120.9 29.3 %all-to-all-start = ((bf16[16,48,768]{2,1,0:T(8,128)(2,1)}), bf16[16,48,768]{2,1,0:T(8,128)(2,1)S(1)}, u32[]{:S(2)}, u32[]{:S(2)}) async-start(bf16[16,48,768]{2,1,0:T(8,128)(2,1)} %bitcast.526), calls=%async_computation | async-start | bytes 2359296 | tf_op jit(solution)/shard_map/all_to_all | solution.py:209
  123.4 299.9 %all-gather.13.cloned.1.call-start = ((), (), s32[]{:S(2)}) async-start(), calls=%async_computation.11 | async-start | bytes 10027008 | tf_op jit(solution)/shard_map/all_gather | solution.py:203
  181.3 61.7 %copy-start.105 = (f32[768]{0:T(1024)}, f32[768]{0:T(1024)S(1)}, u32[]{:S(2)}) copy-start(f32[768]{0:T(1024)S(1)} %get-tuple-element.166) | copy-start | bytes 9220
  186.1 142.3 %copy-start.94 = (f32[768]{0:T(1024)}, f32[768]{0:T(1024)S(1)}, u32[]{:S(2)}) copy-start(f32[768]{0:T(1024)S(1)} %reshape.1031) | copy-start | bytes 9220
  219.0 32.3 %copy-start.2 = (f32[2,384,768]{2,1,0:T(8,128)}, f32[2,384,768]{2,1,0:T(8,128)S(1)}, u32[]{:S(2)}) copy-start(f32[2,384,768]{2,1,0:T(8,128)S(1)} %get-tuple-element.179) | copy-start | bytes 7077892
  219.0 24.0 %copy-start.96 = (f32[2,384]{1,0:T(2,128)}, f32[2,384]{1,0:T(2,128)S(1)}, u32[]{:S(2)}) copy-start(f32[2,384]{1,0:T(2,128)S(1)} %broadcast_multiply_fusion.6) | copy-start | bytes 9220
  220.2 31.1 %copy-start.139 = (f32[3072]{0:T(1024)}, f32[3072]{0:T(1024)S(1)}, u32[]{:S(2)}) copy-start(f32[3072]{0:T(1024)S(1)} %slice_convert_fusion.7) | copy-start | bytes 36868
  222.1 39.5 %copy-start.110 = (f32[768]{0:T(1024)}, f32[768]{0:T(1024)S(1)}, u32[]{:S(2)}) copy-start(f32[768]{0:T(1024)S(1)} %get-tuple-element.163) | copy-start | bytes 9220
  222.1 39.5 %copy-start.151 = (f32[768]{0:T(1024)}, f32[768]{0:T(1024)S(1)}, u32[]{:S(2)}) copy-start(f32[768]{0:T(1024)S(1)} %get-tuple-element.162) | copy-start | bytes 9220
  222.1 94.1 %copy-start.107 = (f32[768]{0:T(1024)}, f32[768]{0:T(1024)S(1)}, u32[]{:S(2)}) copy-start(f32[768]{0:T(1024)S(1)} %get-tuple-element.160) | copy-start | bytes 9220
  268.3 41.1 %copy-start.24 = (bf16[1,2,384,768]{2,3,1,0:T(8,128)(2,1)}, bf16[1,2,384,768]{2,3,1,0:T(8,128)(2,1)S(1)}, u32[]{:S(2)}) copy-start(bf16[1,2,384,768]{2,3,1,0:T(8,128)(2,1)S(1)} %get-tuple-element.123) | copy-start | bytes 3538948
  330.4 395.3 %all-gather.15.cloned.1.call-start = ((), (), s32[]{:S(2)}) async-start(), calls=%async_computation.12 | async-start | bytes 10027008 | tf_op jit(solution)/shard_map/all_gather | solution.py:203
  356.2 67.1 %all-to-all-start.1 = ((bf16[16,48,2560]{2,1,0:T(8,128)(2,1)}), bf16[16,48,2560]{2,1,0:T(8,128)(2,1)}, u32[]{:S(2)}, u32[]{:S(2)}) async-start(bf16[16,48,2560]{2,1,0:T(8,128)(2,1)} %bitcast.482), calls=%async_computation.1 | async-start | bytes 7864320 | tf_op jit(solution)/shard_map/all_to_all | solution.py:209
  359.5 755.7 %reduce-scatter.7.cloned.1.call-start = ((), (), s32[]{:S(2)}) async-start(), calls=%async_computation.13 | async-start | bytes 20054016 | tf_op jit(solution)/shard_map/reduce_scatter | solution.py:206
  725.6 444.5 %reduce-scatter.9.cloned.1.call-start = ((), (), s32[]{:S(2)}) async-start(), calls=%async_computation.14 | async-start | bytes 20054016 | tf_op jit(solution)/shard_map/reduce_scatter | solution.py:206
  1078.1 33.0 %all-to-all-start.3 = ((bf16[16,48,768]{2,1,0:T(8,128)(2,1)}), bf16[16,48,768]{2,1,0:T(8,128)(2,1)S(1)}, u32[]{:S(2)}, u32[]{:S(2)}) async-start(bf16[16,48,768]{2,1,0:T(8,128)(2,1)} %bitcast.525), calls=%async_computation.4 | async-start | bytes 2359296 | tf_op jit(solution)/shard_map/all_to_all | solution.py:209
  1080.7 803.8 %reduce-scatter.13.cloned.1.call-start = ((), (), s32[]{:S(2)}) async-start(), calls=%async_computation.16 | async-start | bytes 10027008 | tf_op jit(solution)/shard_map/reduce_scatter | solution.py:206
  1111.1 61.8 %copy-start.87 = (f32[2,384]{1,0:T(2,128)S(1)}, f32[2,384]{1,0:T(2,128)}, u32[]{:S(2)}) copy-start(f32[2,384]{1,0:T(2,128)} %copy-done.86) | copy-start | bytes 9220
  1111.1 61.8 %copy-start.95 = (f32[768]{0:T(1024)S(1)}, f32[768]{0:T(1024)}, u32[]{:S(2)}) copy-start(f32[768]{0:T(1024)} %copy-done.94) | copy-start | bytes 9220
  1111.1 61.8 %copy-start.104 = (f32[2,384]{1,0:T(2,128)S(1)}, f32[2,384]{1,0:T(2,128)}, u32[]{:S(2)}) copy-start(f32[2,384]{1,0:T(2,128)} %copy-done.103) | copy-start | bytes 9220
  1115.2 57.7 %copy-start.9 = (f32[768,768]{0,1:T(8,128)}, f32[768,768]{0,1:T(8,128)S(1)}, u32[]{:S(2)}) copy-start(f32[768,768]{0,1:T(8,128)S(1)} %copy.247) | copy-start | bytes 7077892
  1266.4 622.6 %reduce-scatter.11.cloned.1.call-start = ((), (), s32[]{:S(2)}) async-start(), calls=%async_computation.15 | async-start | bytes 11698176 | tf_op jit(solution)/shard_map/reduce_scatter | solution.py:206
  1378.4 523.2 %reduce-scatter.17.cloned.1.call-start = ((), (), s32[]{:S(2)}) async-start(), calls=%async_computation.18 | async-start | bytes 20054016 | tf_op jit(solution)/shard_map/reduce_scatter | solution.py:206
  1417.9 487.7 %reduce-scatter.15.cloned.1.call-start = ((), (), s32[]{:S(2)}) async-start(), calls=%async_computation.17 | async-start | bytes 20054016 | tf_op jit(solution)/shard_map/reduce_scatter | solution.py:206
  1620.7 131.2 %all-to-all-start.2 = ((f32[16,48,2560]{2,1,0:T(8,128)}), f32[16,48,2560]{2,1,0:T(8,128)}, u32[]{:S(2)}, u32[]{:S(2)}) async-start(f32[16,48,2560]{2,1,0:T(8,128)} %bitcast.458), calls=%async_computation.2 | async-start | bytes 15728640 | tf_op jit(solution)/shard_map/all_to_all | solution.py:209
  1751.9 55.7 %all-to-all-start.4 = ((f32[16,48,768]{2,1,0:T(8,128)}), f32[16,48,768]{2,1,0:T(8,128)S(1)}, u32[]{:S(2)}, u32[]{:S(2)}) async-start(f32[16,48,768]{2,1,0:T(8,128)} %bitcast.126), calls=%async_computation.6 | async-start | bytes 4718592 | tf_op jit(solution)/shard_map/all_to_all | solution.py:209
  1908.5 42.5 %copy-start.132 = (f32[3,2,624]{2,1,0:T(2,128)S(1)}, f32[3,2,624]{2,1,0:T(2,128)}, u32[]{:S(2)}) copy-start(f32[3,2,624]{2,1,0:T(2,128)} %param.18) | copy-start | bytes 44932
  1909.5 41.6 %copy-start.73 = (f32[1,224,768]{2,1,0:T(8,128)S(1)}, f32[1,224,768]{2,1,0:T(8,128)}, u32[]{:S(2)}) copy-start(f32[1,224,768]{2,1,0:T(8,128)} %reduce-scatter.11.cloned.1.call-done) | copy-start | bytes 2064388
  (170 other events, 990.9 us)
Sparse Core Ops, SparseCore 0:
  13.5 39.4 all-gather.20
  55.8 39.3 all-gather.16
  98.0 59.5 all-gather.18
  159.7 52.1 all-gather.22
  330.5 87.1 all-gather.12
  420.3 55.9 all-gather.14
  725.7 129.9 reduce-scatter.6
  1043.2 126.8 reduce-scatter.8
  1266.6 79.4 reduce-scatter.12
  1378.5 85.0 reduce-scatter.10
  1468.5 114.1 reduce-scatter.16
  1587.4 227.7 reduce-scatter.14

commit v2 on v1

v2 whole, which is shorter than its diff:
```python
import functools

import jax
import jax.numpy as jnp
from jax import lax
from jax.experimental import pallas as pl
from jax.experimental.pallas import tpu as pltpu
from jax.sharding import PartitionSpec as P

NORM_EPS = 1e-5
LEARN_RATE = 3e-3
BETA_ONE = 0.9
BETA_TWO = 0.95
ADAM_EPS = 1e-8
WEIGHT_DECAY = 0.1
CLIP_NORM = 1.0
ADAM_STEP = 10
DECAYS = (WEIGHT_DECAY,) * 6 + (0.0, 0.0)
LANES = 128
TOKEN_TILE = 512
VOCAB_TILE = 512
GRAD_TILE = 640
VMEM_BYTES = 60 * 1024 * 1024


def layer_norm(residual, gain, bias):
    mean_val = jnp.mean(residual, axis=-1, keepdims=True)
    centered = residual - mean_val
    variance = jnp.mean(centered * centered, axis=-1, keepdims=True)
    return centered * lax.rsqrt(variance + NORM_EPS) * gain.astype(jnp.float32) + bias.astype(jnp.float32)


def affine(x, weight, bias):
    return jnp.einsum('bsd,de->bse', x, weight, preferred_element_type=jnp.float32) + bias


def attention_half(residual, wq, wk, wv, proj_t, bq, bk, bv, bo, gain, shift, num_heads):
    batch, seq_len, d_model = residual.shape
    head_dim = d_model // num_heads
    normed_in = layer_norm(residual, gain, shift).astype(jnp.bfloat16)
    q, k, v = (affine(normed_in, w, b).astype(jnp.bfloat16).reshape(batch, seq_len, num_heads, head_dim) for w, b in ((wq, bq), (wk, bk), (wv, bv)))
    scores = jnp.einsum('bqhk,bshk->bhqs', q, k, preferred_element_type=jnp.float32) * head_dim ** -0.5
    rows_iota = lax.broadcasted_iota(jnp.int32, (seq_len, seq_len), 0)
    cols_iota = lax.broadcasted_iota(jnp.int32, (seq_len, seq_len), 1)
    scores = jnp.where(rows_iota >= cols_iota, scores, -1e30)
    attn_prob = jax.nn.softmax(scores, axis=-1).astype(jnp.bfloat16)
    mixed = jnp.einsum('bhqs,bshk->bqhk', attn_prob, v, preferred_element_type=jnp.float32).astype(jnp.bfloat16)
    mixed = mixed.reshape(batch, seq_len, d_model)
    return residual + jnp.einsum('bsl,el->bse', mixed, proj_t, preferred_element_type=jnp.float32) + bo


def feed_half(residual, ups, downs, b1s, b2, gain, shift):
    normed_mid = layer_norm(residual, gain, shift).astype(jnp.bfloat16)
    out = residual + b2
    for up_w, down_w, b1 in zip(ups, downs, b1s):
        hidden = jax.nn.relu(affine(normed_mid, up_w, b1)).astype(jnp.bfloat16)
        out = out + jnp.einsum('bsf,fd->bsd', hidden, down_w, preferred_element_type=jnp.float32)
    return out


def final_norm(residual, lnf_c):
    return layer_norm(residual, lnf_c[0], lnf_c[1]).astype(jnp.bfloat16)


def square_flip(tile):
    fill = jnp.zeros((LANES - tile.shape[0], LANES), jnp.float32)
    return jnp.transpose(jnp.concatenate([tile, fill], axis=0))


def lookup_kernel(ids_ref, blocks_ref, *refs):
    out_refs, (table_ref, rows_ref) = refs[:-2], refs[-2:]
    parts, shard, width = blocks_ref.shape

    def build(j, carry):
        for k in range(width // LANES):
            tile = blocks_ref[j, :, k * LANES:(k + 1) * LANES].astype(jnp.float32)
            table_ref[pl.ds(pl.multiple_of(j * width + k * LANES, LANES), LANES), :] = square_flip(tile)
        return carry

    lax.fori_loop(0, parts, build, 0)
    for which, out_ref in enumerate(out_refs):
        per_part = out_ref.shape[2] // LANES

        def pick(g, carry):
            for v in range(LANES // 8):
                rows = [table_ref[pl.ds(ids_ref[which, g * LANES + v * 8 + u], 1), :] for u in range(8)]
                rows_ref[v * 8:(v + 1) * 8, :] = jnp.concatenate(rows, axis=0)
            flip = jnp.transpose(rows_ref[...])[:shard].astype(jnp.bfloat16)
            out_ref[g // per_part, :, pl.ds(pl.multiple_of(g % per_part * LANES, LANES), LANES)] = flip
            return carry

        lax.fori_loop(0, out_ref.shape[0] * per_part, pick, 0)


def lookup_rows(ids, blocks, tok_dev):
    sets, tokens = ids.shape
    parts, shard, width = blocks.shape
    return pl.pallas_call(
        lookup_kernel,
        out_shape=[jax.ShapeDtypeStruct((parts, shard, tok_dev), jnp.bfloat16)] * sets,
        in_specs=[pl.BlockSpec(memory_space=pltpu.SMEM), pl.BlockSpec(memory_space=pltpu.VMEM)],
        out_specs=[pl.BlockSpec(memory_space=pltpu.VMEM)] * sets,
        scratch_shapes=[pltpu.VMEM((parts * width, LANES), jnp.float32), pltpu.VMEM((LANES, LANES), jnp.float32)],
        compiler_params=pltpu.CompilerParams(vmem_limit_bytes=VMEM_BYTES),
        cost_estimate=pl.CostEstimate(flops=3 * 10 ** 10, bytes_accessed=blocks.size * 2 + sets * tokens * shard * 2, transcendentals=0),
    )(ids, blocks)


def accumulate_kernel(ids_ref, d_ref, low_ref, high_ref, out_ref, sq_ref, acc_ref, rows_ref):
    parts, shard, width = low_ref.shape
    per_part = d_ref.shape[2] // LANES

    def clear(i, carry):
        acc_ref[pl.ds(pl.multiple_of(i * 512, 512), 512), :] = jnp.zeros((512, LANES), jnp.float32)
        return carry

    lax.fori_loop(0, acc_ref.shape[0] // 512, clear, 0)

    def step(g, carry):
        rows_ref[...] = square_flip(d_ref[g // per_part, :, pl.ds(pl.multiple_of(g % per_part * LANES, LANES), LANES)])
        for v in range(LANES // 8):
            rows = rows_ref[v * 8:(v + 1) * 8, :]
            for u in range(8):
                idx = ids_ref[0, g * LANES + v * 8 + u]
                acc_ref[pl.ds(idx, 1), :] = acc_ref[pl.ds(idx, 1), :] + rows[u:u + 1, :]
        return carry

    lax.fori_loop(0, parts * per_part, step, 0)

    def emit(j, total):
        for half, head_ref in enumerate((low_ref, high_ref)):
            for k in range(width // LANES):
                place = pl.ds(pl.multiple_of((2 * j + half) * width + k * LANES, LANES), LANES)
                grad = jnp.transpose(acc_ref[place, :])[:shard] + head_ref[j, :, k * LANES:(k + 1) * LANES]
                out_ref[:, place] = grad
                total = total + grad * grad
        return total

    sq_ref[...] = lax.fori_loop(0, parts, emit, jnp.zeros((shard, LANES), jnp.float32))


def accumulate_rows(ids, d_blocks, head_halves):
    parts, shard, width = head_halves[0].shape
    num_rows = 2 * parts * width
    vmem = pl.BlockSpec(memory_space=pltpu.VMEM)
    return pl.pallas_call(
        accumulate_kernel,
        out_shape=(jax.ShapeDtypeStruct((shard, num_rows), jnp.float32), jax.ShapeDtypeStruct((shard, LANES), jnp.float32)),
        in_specs=[pl.BlockSpec(memory_space=pltpu.SMEM), vmem, vmem, vmem],
        out_specs=(vmem, vmem),
        scratch_shapes=[pltpu.VMEM((num_rows, LANES), jnp.float32), pltpu.VMEM((LANES, LANES), jnp.float32)],
        compiler_params=pltpu.CompilerParams(vmem_limit_bytes=VMEM_BYTES),
        cost_estimate=pl.CostEstimate(flops=5 * 10 ** 10, bytes_accessed=num_rows * shard * 8 + d_blocks.size * 4, transcendentals=0),
    )(ids, d_blocks, *head_halves)


def head_forward_kernel(h_ref, head_ref, mask_ref, u_ref, lse_ref, logit_ref):
    h_tile = h_ref[...]
    slice_len = head_ref.shape[1]
    top = jnp.full((h_tile.shape[0], 1), -jnp.inf, jnp.float32)
    for start in range(0, slice_len, VOCAB_TILE):
        cols = slice(start, start + VOCAB_TILE)
        logits = jnp.dot(h_tile, head_ref[:, cols], preferred_element_type=jnp.float32) + mask_ref[:, cols]
        logit_ref[:, cols] = logits
        top = jnp.maximum(top, jnp.max(logits, axis=-1, keepdims=True))
    total = jnp.zeros_like(top)
    for start in range(0, slice_len, VOCAB_TILE):
        cols = slice(start, start + VOCAB_TILE)
        exp_shift = jnp.exp(logit_ref[:, cols] - top)
        total = total + jnp.sum(exp_shift, axis=-1, keepdims=True)
        part = lax.dot_general(exp_shift.astype(jnp.bfloat16), head_ref[:, cols], (((1,), (1,)), ((), ())), preferred_element_type=jnp.float32)
        if start == 0:
            u_ref[...] = part
        else:
            u_ref[...] += part
    u_ref[...] = u_ref[...] * (1.0 / total)
    lse = top + jnp.log(total)
    lse_ref[...] = jnp.transpose(jnp.broadcast_to(lse, (lse.shape[0], LANES)))[:8]


def head_forward(h_all, head_t, mask):
    tokens, d_model = h_all.shape
    slice_len = head_t.shape[1]
    return pl.pallas_call(
        head_forward_kernel,
        grid=(tokens // TOKEN_TILE,),
        out_shape=(jax.ShapeDtypeStruct((tokens, d_model), jnp.float32), jax.ShapeDtypeStruct((8, tokens), jnp.float32)),
        in_specs=[pl.BlockSpec((TOKEN_TILE, d_model), lambda i: (i, 0)), pl.BlockSpec((d_model, slice_len), lambda i: (0, 0)), pl.BlockSpec((1, slice_len), lambda i: (0, 0))],
        out_specs=(pl.BlockSpec((TOKEN_TILE, d_model), lambda i: (i, 0)), pl.BlockSpec((8, TOKEN_TILE), lambda i: (0, i))),
        scratch_shapes=[pltpu.VMEM((TOKEN_TILE, slice_len), jnp.float32)],
        compiler_params=pltpu.CompilerParams(vmem_limit_bytes=VMEM_BYTES, dimension_semantics=('arbitrary',)),
        cost_estimate=pl.CostEstimate(flops=4 * tokens * d_model * slice_len, bytes_accessed=tokens * d_model * 6 + head_t.size * 2, transcendentals=tokens * slice_len),
    )(h_all, head_t, mask)


def as_column(row):
    return jnp.transpose(jnp.broadcast_to(row, (LANES, row.shape[1])))[:, :1]


def head_grad_kernel(inv_tokens, origin, h_ref, head_ref, mask_ref, lse_ref, tgt_ref, *refs):
    init_ref, grad_ref, flip_ref = refs if len(refs) == 3 else (None,) + refs
    h_tile = h_ref[...]
    width = head_ref.shape[1]
    flip_ref[...] = jnp.transpose(h_tile)
    lse = as_column(lse_ref[...])
    tgt = as_column(tgt_ref[...]).astype(jnp.int32)

    @pl.when(pl.program_id(0) == 0)
    def _():
        grad_ref[...] = jnp.zeros_like(grad_ref) if init_ref is None else init_ref[...]

    for start in range(0, width, GRAD_TILE):
        cols = slice(start, start + GRAD_TILE)
        logits = jnp.dot(h_tile, head_ref[:, cols], preferred_element_type=jnp.float32) + mask_ref[:, cols]
        prob = jnp.exp(logits - lse) * inv_tokens
        is_target = lax.broadcasted_iota(jnp.int32, logits.shape, 1) == tgt - (origin + start)
        d_logits = jnp.where(is_target, prob - inv_tokens, prob).astype(jnp.bfloat16)
        grad_ref[:, cols] += jnp.dot(flip_ref[...], d_logits, preferred_element_type=jnp.float32)


def head_grad(h_all, head_t, mask, lse, tgt, init, inv_tokens, half):
    tokens, d_model = h_all.shape
    slice_len = head_t.shape[1]
    width = slice_len // 2
    whole = pl.BlockSpec((d_model, width), lambda i: (0, 0))
    row = pl.BlockSpec((1, TOKEN_TILE), lambda i: (0, i))
    extra = () if init is None else (init,)
    return pl.pallas_call(
        functools.partial(head_grad_kernel, inv_tokens, half * width),
        grid=(tokens // TOKEN_TILE,),
        out_shape=jax.ShapeDtypeStruct((d_model, width), jnp.float32),
        in_specs=[pl.BlockSpec((TOKEN_TILE, d_model), lambda i: (i, 0)), pl.BlockSpec((d_model, width), lambda i: (0, half)), pl.BlockSpec((1, width), lambda i: (0, half)), row, row] + [whole] * len(extra),
        out_specs=whole,
        scratch_shapes=[pltpu.VMEM((d_model, TOKEN_TILE), jnp.bfloat16)],
        compiler_params=pltpu.CompilerParams(vmem_limit_bytes=VMEM_BYTES, dimension_semantics=('arbitrary',)),
        cost_estimate=pl.CostEstimate(flops=4 * tokens * d_model * width, bytes_accessed=tokens * d_model * 2 + head_t.size * 3, transcendentals=tokens * width),
    )(h_all, head_t, mask, lse, tgt, *extra)


def adam_update(state, grad, decay):
    moment = BETA_ONE * state[1] + (1.0 - BETA_ONE) * grad
    second = BETA_TWO * state[2] + (1.0 - BETA_TWO) * grad * grad
    m_hat = moment / (1.0 - BETA_ONE ** ADAM_STEP)
    v_hat = second / (1.0 - BETA_TWO ** ADAM_STEP)
    master = state[0] * (1.0 - LEARN_RATE * decay) - LEARN_RATE * m_hat / (jnp.sqrt(v_hat) + ADAM_EPS)
    return jnp.stack([master, moment, second])


def solution(mesh):
    n_dev = mesh.shape['dp']
    row_spec = P('dp', None)
    state_specs = (P(None, None, 'dp'), P(None, None, 'dp'), P(None, None, 'dp', None, None, None), P(None, None, None, None, 'dp'), P(None, None, 'dp', None), P(None, None, 'dp', None), P(None, None, 'dp'), P(None, None, 'dp'))

    def gather(local):
        return lax.all_gather(local, 'dp', axis=0, tiled=False)

    def scatter_sum(full):
        return lax.psum_scatter(full, 'dp', scatter_dimension=0, tiled=False)

    def swap(blocks):
        return lax.all_to_all(blocks, 'dp', split_axis=0, concat_axis=0, tiled=False)

    def train_step(token_ids, target_ids, st_wte, st_wpe, st_qkv, st_proj, st_up, st_down, st_vec, st_lnf):
        num_layers, shard = st_qkv.shape[1], st_qkv.shape[2]
        num_heads = st_qkv.shape[4]
        batch_dev, seq_len = token_ids.shape
        vocab_size = st_wte.shape[1]
        pos_rows = st_wpe.shape[1]
        d_model = shard * n_dev
        ff_shard = st_down.shape[2]
        ff_dim = ff_shard * n_dev
        ff_parts = ff_dim // d_model
        vec_shard = st_vec.shape[2]
        tok_dev = batch_dev * seq_len
        tokens = tok_dev * n_dev
        inv_tokens = 1.0 / tokens
        slice_len = -(-vocab_size // (n_dev * VOCAB_TILE)) * VOCAB_TILE
        vocab_pad = slice_len * n_dev
        me = lax.axis_index('dp')

        head_send = jnp.pad(st_wte[0].T.astype(jnp.bfloat16), ((0, 0), (0, vocab_pad - vocab_size)))
        head_send = jnp.swapaxes(head_send.reshape(shard, n_dev, slice_len), 0, 1)
        ids_all = lax.all_gather(jnp.stack([token_ids, target_ids]), 'dp', axis=1, tiled=True).reshape(2, tokens)
        token_send, target_send = lookup_rows(ids_all, head_send, tok_dev)
        token_rows = swap(token_send).reshape(d_model, tok_dev).T.astype(jnp.float32)

        def half_pack(parts):
            return jnp.concatenate([part.astype(jnp.bfloat16) for part in parts], axis=0)

        pos_pack = st_wpe[0, 2:2 + seq_len].T.reshape(-1, d_model)
        pos_count = pos_pack.shape[0]
        small_rows = jnp.concatenate([st_vec[0], jnp.pad(st_lnf[0].reshape(1, -1), ((0, 0), (0, vec_shard - 2 * shard)))], axis=0)
        small_rows = jnp.pad(small_rows, ((0, (-(num_layers + 1 + pos_count)) % 16), (0, d_model - vec_shard)))
        packs = []
        for layer in range(num_layers):
            qkv = st_qkv[0, layer].reshape(shard, 3, d_model)
            parts = [qkv[:, 0], qkv[:, 1], qkv[:, 2], st_proj[0, layer].reshape(d_model, shard).T]
            packs.append(half_pack(parts + ([pos_pack, small_rows] if layer == 0 else [])))
            packs.append(half_pack([st_up[0, layer, :, c * d_model:(c + 1) * d_model] for c in range(ff_parts)] + [st_down[0, layer]]))
        gathered = [gather(pack) for pack in packs]
        attn_rows = 4 * shard
        first = gathered[0]
        pos_c = first[:, attn_rows:attn_rows + pos_count].reshape(d_model, seq_len).T.astype(jnp.float32)
        small_c = first[:, attn_rows + pos_count:attn_rows + pos_count + num_layers + 1, :vec_shard].astype(jnp.float32)
        lnf_c = jnp.swapaxes(small_c[:, num_layers, :2 * shard].reshape(n_dev, 2, shard), 0, 1).reshape(2, d_model)
        group = n_dev // ff_parts

        residual = token_rows.reshape(batch_dev, seq_len, d_model) + pos_c
        attn_backs, feed_backs = [], []
        for layer in range(num_layers):
            vec = small_c[:, layer].reshape(-1, d_model)
            wts = [gathered[2 * layer][:, c * shard:(c + 1) * shard].reshape(d_model, d_model) for c in range(4)]
            residual, back = jax.vjp(functools.partial(attention_half, num_heads=num_heads), residual, *wts, vec[0], vec[1], vec[2], vec[3], vec[5 + ff_parts], vec[6 + ff_parts])
            attn_backs.append(back)
            feed = gathered[2 * layer + 1]
            ups = tuple(feed[:, c * shard:(c + 1) * shard].reshape(d_model, d_model) for c in range(ff_parts))
            downs = tuple(feed[c * group:(c + 1) * group, ff_parts * shard:].reshape(d_model, d_model) for c in range(ff_parts))
            b1s = tuple(vec[4 + c] for c in range(ff_parts))
            residual, back = jax.vjp(feed_half, residual, ups, downs, b1s, vec[4 + ff_parts], vec[7 + ff_parts], vec[8 + ff_parts])
            feed_backs.append(back)
            if layer == 0:
                head_t = swap(head_send)
                residual, head_t = lax.optimization_barrier((residual, head_t))
                head_t = head_t.reshape(d_model, slice_len)
        normed, norm_back = jax.vjp(final_norm, residual, lnf_c)

        vocab_pos = me * slice_len + lax.broadcasted_iota(jnp.int32, (1, slice_len), 1)
        mask = jnp.where(vocab_pos < vocab_size, 0.0, -1e30).astype(jnp.float32)
        tgt_local = (ids_all[1] - me * slice_len).astype(jnp.float32).reshape(n_dev, batch_dev, seq_len)
        h_alls = [gather(normed[row]).reshape(n_dev * seq_len, d_model) for row in range(batch_dev)]
        target_rows = swap(target_send).reshape(d_model, tok_dev).T.astype(jnp.float32).reshape(batch_dev, seq_len, d_model)
        lse_alls, d_sums, loss_part = [], [], 0.0
        for row in range(batch_dev):
            u_part, lse_part = head_forward(h_alls[row], head_t, mask)
            lse_part = lse_part[0].reshape(-1, LANES)
            lse_dev = gather(lse_part)
            top = jnp.max(lse_dev, axis=0)
            lse = top + jnp.log(jnp.sum(jnp.exp(lse_dev - top), axis=0))
            factor = (jnp.exp(lse_part - lse) * inv_tokens).reshape(n_dev, seq_len, 1)
            scaled = u_part.reshape(n_dev, seq_len, d_model) * factor
            if row + 1 < batch_dev:
                scaled, h_alls[row + 1] = lax.optimization_barrier((scaled, h_alls[row + 1]))
            d_sums.append(scatter_sum(scaled))
            lse_alls.append(lse.reshape(1, -1))
            own = lax.dynamic_slice_in_dim(lse.reshape(n_dev, seq_len), me, 1, axis=0)
            picked = jnp.sum(normed[row].astype(jnp.float32) * target_rows[row], axis=-1)
            loss_part = loss_part + (jnp.sum(own) - jnp.sum(picked)) * inv_tokens
        grad_heads = []
        for half in range(2):
            part = None
            for row in range(batch_dev):
                part = head_grad(h_alls[row], head_t, mask, lse_alls[row], tgt_local[:, row].reshape(1, -1), part, inv_tokens, half)
            grad_heads.append(part.reshape(n_dev, shard, slice_len // 2))
        grad_heads[0] = swap(grad_heads[0])
        d_sums, grad_heads = lax.optimization_barrier((d_sums, grad_heads))
        grad_heads[1] = swap(grad_heads[1])
        d_normed = jnp.stack(d_sums) - inv_tokens * target_rows

        d_resid, d_lnf = norm_back(d_normed.astype(jnp.bfloat16))
        vec_rows = [None] * num_layers
        qkv_g, proj_g, up_g, down_g = ([None] * num_layers for _ in range(4))
        feed_rows = attn_rows + ff_parts * shard
        for layer in reversed(range(num_layers)):
            d_resid, d_ups, d_downs, d_b1s, d_b2, d_gain2, d_shift2 = feed_backs[layer](d_resid)
            if layer == num_layers - 1:
                d_resid, grad_heads = lax.optimization_barrier((d_resid, grad_heads))
            d_resid, d_q, d_k, d_v, d_proj, d_bq, d_bk, d_bv, d_bo, d_gain1, d_shift1 = attn_backs[layer](d_resid)
            vec_rows[layer] = jnp.stack([d_bq, d_bk, d_bv, d_bo, *d_b1s, d_b2, d_gain1, d_shift1, d_gain2, d_shift2]).reshape(n_dev, 1, vec_shard)
            parts = [g.reshape(n_dev, shard, d_model) for g in (d_q, d_k, d_v, d_proj, *d_ups)]
            parts.append(jnp.concatenate([g.reshape(group, ff_shard, d_model) for g in d_downs], axis=0))
            parts = [part.astype(jnp.float32) for part in parts]
            if layer == 0:
                pos_sum = jnp.sum(d_resid, axis=0).T.reshape(n_dev, pos_count, d_model)
                rows = jnp.pad(jnp.swapaxes(d_lnf.reshape(2, n_dev, shard), 0, 1).reshape(n_dev, 1, 2 * shard), ((0, 0), (0, 0), (0, vec_shard - 2 * shard)))
                rows = jnp.concatenate(vec_rows + [rows], axis=1)
                rows = jnp.pad(rows, ((0, 0), (0, (-(num_layers + 1 + pos_count)) % 8), (0, d_model - vec_shard)))
                parts = parts + [pos_sum, rows]
            summed = scatter_sum(jnp.concatenate(parts, axis=1))
            qkv_g[layer] = jnp.swapaxes(summed[:3 * shard].reshape(3, shard, d_model), 0, 1).reshape(st_qkv.shape[2:])
            proj_g[layer] = summed[3 * shard:attn_rows].T.reshape(st_proj.shape[2:])
            up_g[layer] = jnp.swapaxes(summed[attn_rows:feed_rows].reshape(ff_parts, shard, d_model), 0, 1).reshape(shard, ff_dim)
            down_g[layer] = summed[feed_rows:feed_rows + ff_shard]
            if layer == 0:
                tail = feed_rows + ff_shard
                pos_g = jnp.pad(summed[tail:tail + pos_count].reshape(shard, seq_len).T, ((2, pos_rows - 2 - seq_len), (0, 0)))
                small_g = summed[tail + pos_count:tail + pos_count + num_layers + 1, :vec_shard]
        vec_g = small_g[:num_layers]
        lnf_g = small_g[num_layers, :2 * shard].reshape(2, shard)

        lookup_d = swap(d_resid.reshape(tok_dev, d_model).T.reshape(n_dev, shard, tok_dev))
        wte_g, wte_sq = accumulate_rows(ids_all, lookup_d, grad_heads)

        grads = [pos_g, jnp.stack(qkv_g), jnp.stack(proj_g), jnp.stack(up_g), jnp.stack(down_g), vec_g, lnf_g]
        local_sq = jnp.sum(wte_sq) + sum(jnp.sum(grad * grad) for grad in grads)
        sums = lax.psum(jnp.stack([local_sq, loss_part]), 'dp')
        clip_coef = jnp.minimum(1.0, CLIP_NORM / (jnp.sqrt(sums[0]) + 1e-6))
        new_wte = jnp.swapaxes(adam_update(jnp.swapaxes(st_wte, 1, 2), wte_g[:, :vocab_size] * clip_coef, DECAYS[0]), 1, 2)
        states = (st_wpe, st_qkv, st_proj, st_up, st_down, st_vec, st_lnf)
        new_states = tuple(adam_update(state, grad * clip_coef, decay) for state, grad, decay in zip(states, grads, DECAYS[1:]))
        return (sums[1], new_wte) + new_states

    return jax.shard_map(train_step, mesh=mesh, in_specs=(row_spec, row_spec) + state_specs, out_specs=(P(),) + state_specs, check_vma=False)
```

time: 2100 us -> 1420 us (0.68)
  blocking collectives: 422 us -> 74.1 us
  other arithmetic: 342 us -> 191 us
  local copies, waits for them, and re-layouts: 365 us -> 235 us
  waiting for transfers between devices: 293 us -> 168 us
  Pallas kernels: 401 us -> 466 us
    all_gather x2, blocking collectives: 373 us -> 26.9 us  [gather(): return lax.all_gather(local, 'dp', axis=0, tiled=False)]
    all_to_all x5 -> x6, waiting for transfers between devices: 237 us -> 93.2 us  [swap(): lax.all_to_all(blocks, 'dp', split_axis=0, concat_axis=0, tiled=False)]
    pallas_call x5 -> x6, Pallas kernels: 248 us -> 314 us  [the longest x4 172 us: head_grad(): pl.pallas_call(functools.partial(head_grad_kernel, inv_tokens, half * wid...]
    all_gather x6, waiting for transfers between devices: 0.06 us -> 52.3 us  [gather(): return lax.all_gather(local, 'dp', axis=0, tiled=False)]
    all_gather x2 -> x0, other arithmetic: 46.1 us -> none  [train_step(): lse_dev = lax.all_gather(lse_part.reshape(-1), 'dp', axis=0, tiled=False)]
    another operation x11 -> x10, other arithmetic: 71.2 us -> 26.8 us  [adam_update(): return jnp.stack([master, moment, second])]
    reshape x17 -> x7, local copies, waits for them, and re-layouts: 48.5 us -> 8.57 us  [the longest x2 3.06 us: train_step(): jnp.stack([d_bq, d_bk, d_bv, d_bo, *d_b1s, d_b2, d_gain1, d_shift1, d_gai...]
    transpose x9 -> x1, local copies, waits for them, and re-layouts: 39.9 us -> 0.62 us  [train_step(): jnp.swapaxes(d_lnf.reshape(2, n_dev, shard), 0, 1)]
  transfers between devices with their start and end apart: 17 -> 16, of which waited for: 5 -> 6; matrix products, arithmetic and copies ran while one was open for 30% -> 27% of each run, Pallas kernels for 19% -> 33%
where the time goes in v2:
time: 1420 us; the launch traced here: 1410 us
  Pallas kernels  466 us (33%)
  local copies, waits for them, and re-layouts  235 us (17%)
  matrix products  226 us (16%)
  other arithmetic  191 us (13%)
  waiting for transfers between devices  168 us (12%)
  blocking collectives  74.1 us (5%)
  between operations  25.9 us (2%)
  starting transfers between devices  21.7 us (2%)
    pallas_call x4, Pallas kernels, head_grad(): pl.pallas_call(functools.partial(head_grad_kernel, inv_tokens, half * wid...  172 us
    pallas_call x2, Pallas kernels, head_forward(): pl.pallas_call(head_forward_kernel, grid=(tokens // TOKEN_TILE,), out_sha...  152 us
    all_to_all x6, waiting for transfers between devices, swap(): lax.all_to_all(blocks, 'dp', split_axis=0, concat_axis=0, tiled=False)  93.2 us
    dot_general x42, matrix products, affine(): jnp.einsum('bsd,de->bse', x, weight, preferred_element_type=jnp.float32)  84.4 us
    pallas_call x1, Pallas kernels, accumulate_rows(): pl.pallas_call(accumulate_kernel, out_shape=(jax.ShapeDtypeStruct((shard,...  77.7 us
    pallas_call x1, Pallas kernels, lookup_rows(): pl.pallas_call(lookup_kernel, out_shape=[jax.ShapeDtypeStruct((parts, sha...  64.2 us
    unnamed x610, local copies, waits for them, and re-layouts  59.9 us
    all_gather x6, waiting for transfers between devices, gather(): return lax.all_gather(local, 'dp', axis=0, tiled=False)  52.3 us
  transfers between devices with their start and end apart: 16, of which 6 were waited for; matrix products, arithmetic and copies ran while one was open for 27% of the time, Pallas kernels for 33%

profile of v2, /device:TPU:0, one launch (start us, length us, event | category | flops | bytes accessed | tf_op | source)
XLA Modules:
  0.0 1408.9 jit_solution(7750570626169205606)
XLA Ops:
  43.8 15.0 %all_gather.39 = s32[2,32,384]{2,0,1:T(2,128)} all-gather(s32[2,2,384]{2,0,1:T(2,128)S(1)} %pad_add_fusion), channel_id=1, replica_groups=mesh['dp'=16] {'dp'}, dimensions={1}, use_global_device_ids=true | all-gather | bytes 104448 | tf_op jit(solution)/shard_map/all_gather | solution.py:283
  58.8 64.2 %shard_map.169 = (bf16[16,48,768]{2,1,0:T(8,128)(2,1)}, bf16[16,48,768]{2,1,0:T(8,128)(2,1)}) custom-call(s32[2,12288]{1,0:T(2,128)} %bitcast.764, bf16[16,48,2560]{2,1,0:T(8,128)(2,1)} %bitcast.623), custom_call_target="tpu_custom_call" | custom-call | flops 30000001024 | bytes 6291456 | tf_op jit(solution)/shard_map/pallas_call | solution.py:98
  126.1 27.7 %all-to-all-done = bf16[16,48,768]{2,1,0:T(8,128)(2,1)S(1)} async-done(((bf16[16,48,768]{2,1,0:T(8,128)(2,1)}), bf16[16,48,768]{2,1,0:T(8,128)(2,1)S(1)}, u32[]{:S(2)}, u32[]{:S(2)}) %all-to-all-start) | async-done | bytes 1179680 | tf_op jit(solution)/shard_map/all_to_all | solution.py:261
  203.2 10.1 fusion.238
  213.3 9.7 divide_convert_fusion.1
  287.4 9.8 fusion.240
  297.2 9.5 divide_convert_fusion
  335.0 52.2 %all-gather.11.cloned.1.call-done = bf16[16,384,768]{2,1,0:T(8,128)(2,1)} async-done(((bf16[1,384,768]{2,1,0:T(8,128)(2,1)}), bf16[16,384,768]{2,1,0:T(8,128)(2,1)}) %all-gather.11.cloned.1.call-update) | async-done | bytes 9437200 | tf_op jit(solution)/shard_map/all_gather | solution.py:255
  387.2 76.0 %shard_map.170 = (f32[6144,768]{1,0:T(8,128)}, f32[8,6144]{1,0:T(8,128)}) custom-call(bf16[6144,768]{1,0:T(8,128)(2,1)} %bitcast.779, bf16[768,2560]{1,0:T(8,128)(2,1)} %bitcast.95.head_ref, f32[1,2560]{1,0:T(1,128)} %compare_select_fusion.mask_ref), custom_call_target="tpu_custom_call" | custom-call | flops 48318382080 | bytes 32243712 | tf_op jit(solution)/shard_map/pallas_call | solution.py:184
  464.2 13.4 all_gather.49
  477.8 12.6 broadcast_multiply_fusion.1
  490.5 76.1 %shard_map.171 = (f32[6144,768]{1,0:T(8,128)}, f32[8,6144]{1,0:T(8,128)}) custom-call(bf16[6144,768]{1,0:T(8,128)(2,1)} %bitcast.782, bf16[768,2560]{1,0:T(8,128)(2,1)} %bitcast.95.head_ref, f32[1,2560]{1,0:T(1,128)} %compare_select_fusion.mask_ref), custom_call_target="tpu_custom_call" | custom-call | flops 48318382080 | bytes 32243712 | tf_op jit(solution)/shard_map/pallas_call | solution.py:184
  567.6 13.5 all_gather.51
  581.3 12.8 broadcast_multiply_fusion
  597.7 20.5 %all-to-all-done.3 = bf16[16,48,768]{2,1,0:T(8,128)(2,1)S(1)} async-done(((bf16[16,48,768]{2,1,0:T(8,128)(2,1)}), bf16[16,48,768]{2,1,0:T(8,128)(2,1)S(1)}, u32[]{:S(2)}, u32[]{:S(2)}) %all-to-all-start.3) | async-done | bytes 1179680 | tf_op jit(solution)/shard_map/all_to_all | solution.py:261
  629.0 42.3 %shard_map.172.refs_0_ = f32[768,1280]{1,0:T(8,128)} custom-call(bf16[6144,768]{1,0:T(8,128)(2,1)} %bitcast.780, bf16[768,2560]{1,0:T(8,128)(2,1)} %bitcast.95.head_ref, f32[1,2560]{1,0:T(1,128)} %compare_select_fusion.mask_ref, f32[1,6144]{1,0:T(1,128)} %bitcast.768, f32[1,6144]{1,0:T(1,128)} %bitcast.776), custom_call_target="tpu_custom_call" | custom-call | flops 24159191040 | bytes 15335424 | tf_op jit(solution)/shard_map/pallas_call | solution.py:228
  671.3 43.6 %shard_map.173 = f32[768,1280]{1,0:T(8,128)} custom-call(bf16[6144,768]{1,0:T(8,128)(2,1)} %bitcast.783, bf16[768,2560]{1,0:T(8,128)(2,1)} %bitcast.95.head_ref, f32[1,2560]{1,0:T(1,128)} %compare_select_fusion.mask_ref, f32[1,6144]{1,0:T(1,128)} %bitcast.770, f32[1,6144]{1,0:T(1,128)} %bitcast.774, f32[768,1280]{1,0:T(8,128)} %shard_map.172.refs_0_), custom_call_target="tpu_custom_call" | custom-call | flops 24159191040 | bytes 15335424 | tf_op jit(solution)/shard_map/pallas_call | solution.py:228
  718.4 42.3 %shard_map.174.refs_0_ = f32[768,1280]{1,0:T(8,128)} custom-call(bf16[6144,768]{1,0:T(8,128)(2,1)} %bitcast.781, bf16[768,2560]{1,0:T(8,128)(2,1)} %bitcast.95.head_ref, f32[1,2560]{1,0:T(1,128)} %compare_select_fusion.mask_ref, f32[1,6144]{1,0:T(1,128)} %bitcast.769, f32[1,6144]{1,0:T(1,128)} %bitcast.777), custom_call_target="tpu_custom_call" | custom-call | flops 24159191040 | bytes 15335424 | tf_op jit(solution)/shard_map/pallas_call | solution.py:228
  760.7 44.0 %shard_map.175 = f32[768,1280]{1,0:T(8,128)} custom-call(bf16[6144,768]{1,0:T(8,128)(2,1)} %bitcast.784, bf16[768,2560]{1,0:T(8,128)(2,1)} %bitcast.95.head_ref, f32[1,2560]{1,0:T(1,128)} %compare_select_fusion.mask_ref, f32[1,6144]{1,0:T(1,128)} %bitcast.771, f32[1,6144]{1,0:T(1,128)} %bitcast.775, f32[768,1280]{1,0:T(8,128)} %shard_map.174.refs_0_), custom_call_target="tpu_custom_call" | custom-call | flops 24159191040 | bytes 15335424 | tf_op jit(solution)/shard_map/pallas_call | solution.py:228
  853.9 26.6 %all-to-all-done.4.high_ref = f32[16,48,1280]{2,1,0:T(8,128)} async-done(((f32[16,48,1280]{2,1,0:T(8,128)}), f32[16,48,1280]{2,1,0:T(8,128)}, u32[]{:S(2)}, u32[]{:S(2)}) %all-to-all-start.4) | async-done | bytes 3932192 | tf_op jit(solution)/shard_map/all_to_all | solution.py:261
  890.8 8.5 fusion.7
  899.4 12.5 convert_reduce_fusion.6
  932.2 9.7 concatenate.92
  999.3 8.7 fusion.13
  1008.0 10.6 convert_reduce_fusion.9
  1025.4 8.0 convert_reduce_fusion.10
  1134.6 18.3 %all-to-all-done.5.d_ref = f32[16,48,768]{2,1,0:T(8,128)} async-done(((f32[16,48,768]{2,1,0:T(8,128)}), f32[16,48,768]{2,1,0:T(8,128)}, u32[]{:S(2)}, u32[]{:S(2)}) %all-to-all-start.5) | async-done | bytes 2359328 | tf_op jit(solution)/shard_map/all_to_all | solution.py:261
  1152.9 77.7 %shard_map.176 = (f32[48,40960]{1,0:T(8,128)}, f32[48,128]{1,0:T(8,128)}) custom-call(s32[2,12288]{1,0:T(2,128)} %bitcast.765, f32[16,48,768]{2,1,0:T(8,128)} %all-to-all-done.5.d_ref, f32[16,48,1280]{2,1,0:T(8,128)} %all-to-all-done.2.low_ref, f32[16,48,1280]{2,1,0:T(8,128)} %all-to-all-done.4.high_ref), custom_call_target="tpu_custom_call" | custom-call | flops 49999998976 | bytes 18087936 | tf_op jit(solution)/shard_map/pallas_call | solution.py:146
  1251.5 21.8 %reduce-scatter.9.cloned.1.call-done = f32[1,608,768]{2,1,0:T(8,128)} async-done(((f32[16,608,768]{2,1,0:T(8,128)}), f32[1,608,768]{2,1,0:T(8,128)}) %reduce-scatter.9.cloned.1.call-update) | async-done | bytes 1867792 | tf_op jit(solution)/shard_map/reduce_scatter | solution.py:258
  1315.1 32.3 %psum.7 = f32[2]{0:T(128)} all-reduce(f32[2]{0:T(128)} %pad_maximum_fusion.9), channel_id=1, replica_groups=mesh['dp'=16] {'dp'}, use_global_device_ids=true, to_apply=%region_75.76 | all-reduce | flops 2 | bytes 16 | tf_op jit(solution)/shard_map/psum | solution.py:395
  1366.5 16.3 %fusion.22 = (f32[1,48,40478]{2,1,0:T(8,128)S(1)}, f32[1,48,40478]{2,1,0:T(8,128)S(1)}, f32[1,48,40478]{2,1,0:T(8,128)}) fusion(f32[3,48,40478]{2,1,0:T(8,128)} %bitcast.617, f32[]{:T(128)} %bitcast.238, f32[48,40960]{1,0:T(8,128)} %get-tuple-element.46), kind=kLoop, calls=%fused_computation.40 | loop fusion | flops 27201216 | bytes 54402436 | tf_op jit(solution)/shard_map/stack | solution.py:246
  1387.5 8.3 maximum_bitcast_fusion
  (972 shorter events, 528.5 us)
Async XLA Ops:
  7.2 153.9 %all-gather.19.cloned.1.call-start = ((), (), s32[]{:S(2)}) async-start(), calls=%async_computation.18 | async-start | bytes 5013504 | tf_op jit(solution)/shard_map/all_gather | solution.py:255
  11.8 21.9 %copy-start.15 = (f32[3,2,48,3072]{3,2,1,0:T(8,128)S(1)}, f32[3,2,48,3072]{3,2,1,0:T(8,128)}, u32[]{:S(2)}) copy-start(f32[3,2,48,3072]{3,2,1,0:T(8,128)} %param.16) | copy-start | bytes 10616836
  13.6 153.0 %all-gather.15.cloned.1.call-start = ((), (), s32[]{:S(2)}) async-start(), calls=%async_computation.16 | async-start | bytes 5849088 | tf_op jit(solution)/shard_map/all_gather | solution.py:255
  33.7 197.3 %all-gather.17.cloned.1.call-start = ((), (), s32[]{:S(2)}) async-start(), calls=%async_computation.17 | async-start | bytes 10027008 | tf_op jit(solution)/shard_map/all_gather | solution.py:255
  36.9 212.5 %all-gather.21.cloned.1.call-start = ((), (), s32[]{:S(2)}) async-start(), calls=%async_computation.19 | async-start | bytes 10027008 | tf_op jit(solution)/shard_map/all_gather | solution.py:255
  123.0 30.9 %all-to-all-start = ((bf16[16,48,768]{2,1,0:T(8,128)(2,1)}), bf16[16,48,768]{2,1,0:T(8,128)(2,1)S(1)}, u32[]{:S(2)}, u32[]{:S(2)}) async-start(bf16[16,48,768]{2,1,0:T(8,128)(2,1)} %get-tuple-element.28), calls=%async_computation | async-start | bytes 2359296 | tf_op jit(solution)/shard_map/all_to_all | solution.py:261
  153.8 114.3 %all-to-all-start.1 = ((bf16[16,48,2560]{2,1,0:T(8,128)(2,1)}), bf16[16,48,2560]{2,1,0:T(8,128)(2,1)}, u32[]{:S(2)}, u32[]{:S(2)}) async-start(bf16[16,48,2560]{2,1,0:T(8,128)(2,1)} %bitcast.624), calls=%async_computation.1 | async-start | bytes 7864320 | tf_op jit(solution)/shard_map/all_to_all | solution.py:261
  157.1 230.1 %all-gather.11.cloned.1.call-start = ((), (), s32[]{:S(2)}) async-start(), calls=%async_computation.10 | async-start | bytes 10027008 | tf_op jit(solution)/shard_map/all_gather | solution.py:255
  161.1 66.6 %copy-start.2 = (f32[768,768]{0,1:T(8,128)}, f32[768,768]{0,1:T(8,128)S(1)}, u32[]{:S(2)}) copy-start(f32[768,768]{0,1:T(8,128)S(1)} %copy.249) | copy-start | bytes 7077892
  173.8 53.9 %copy-start.11 = (f32[768,384]{0,1:T(8,128)}, f32[768,384]{0,1:T(8,128)S(1)}, u32[]{:S(2)}) copy-start(f32[768,384]{0,1:T(8,128)S(1)} %copy.252) | copy-start | bytes 3538948
  176.2 54.3 %copy-start.173 = (f32[768]{0:T(1024)}, f32[768]{0:T(1024)S(1)}, u32[]{:S(2)}) copy-start(f32[768]{0:T(1024)S(1)} %get-tuple-element.114) | copy-start | bytes 9220
  201.3 130.4 %copy-start.183 = (f32[768]{0:T(1024)}, f32[768]{0:T(1024)S(1)}, u32[]{:S(2)}) copy-start(f32[768]{0:T(1024)S(1)} %mul.1041) | copy-start | bytes 9220
  203.2 66.3 %copy-start.179 = (f32[768]{0:T(1024)}, f32[768]{0:T(1024)S(1)}, u32[]{:S(2)}) copy-start(f32[768]{0:T(1024)S(1)} %get-tuple-element.108) | copy-start | bytes 9220
  203.2 109.6 %copy-start.181 = (f32[768]{0:T(1024)}, f32[768]{0:T(1024)S(1)}, u32[]{:S(2)}) copy-start(f32[768]{0:T(1024)S(1)} %get-tuple-element.101) | copy-start | bytes 9220
  268.1 43.0 %copy-start = (f32[2,384,768]{2,1,0:T(8,128)}, f32[2,384,768]{2,1,0:T(8,128)S(1)}, u32[]{:S(2)}) copy-start(f32[2,384,768]{2,1,0:T(8,128)S(1)} %add_add_fusion.11) | copy-start | bytes 7077892
  274.8 32.0 %copy-start.20 = (bf16[2,384,768]{1,2,0:T(8,128)(2,1)}, bf16[2,384,768]{1,2,0:T(8,128)(2,1)S(1)}, u32[]{:S(2)}) copy-start(bf16[2,384,768]{1,2,0:T(8,128)(2,1)S(1)} %copy.260) | copy-start | bytes 3538948
  333.7 156.7 %all-gather.13.cloned.1.call-start = ((), (), s32[]{:S(2)}) async-start(), calls=%async_computation.11 | async-start | bytes 10027008 | tf_op jit(solution)/shard_map/all_gather | solution.py:255
  334.3 470.4 %reduce-scatter.5.cloned.1.call-start = ((), (), s32[]{:S(2)}) async-start(), calls=%async_computation.12 | async-start | bytes 20054016 | tf_op jit(solution)/shard_map/reduce_scatter | solution.py:258
  490.5 314.2 %reduce-scatter.7.cloned.1.call-start = ((), (), s32[]{:S(2)}) async-start(), calls=%async_computation.13 | async-start | bytes 20054016 | tf_op jit(solution)/shard_map/reduce_scatter | solution.py:258
  594.1 24.2 %all-to-all-start.3 = ((bf16[16,48,768]{2,1,0:T(8,128)(2,1)}), bf16[16,48,768]{2,1,0:T(8,128)(2,1)S(1)}, u32[]{:S(2)}, u32[]{:S(2)}) async-start(bf16[16,48,768]{2,1,0:T(8,128)(2,1)} %get-tuple-element.39), calls=%async_computation.5 | async-start | bytes 2359296 | tf_op jit(solution)/shard_map/all_to_all | solution.py:261
  622.0 184.5 %copy-start.13 = (f32[768,768]{0,1:T(8,128)}, f32[768,768]{0,1:T(8,128)S(1)}, u32[]{:S(2)}) copy-start(f32[768,768]{0,1:T(8,128)S(1)} %copy.267) | copy-start | bytes 7077892
  623.3 195.8 %copy-start.130 = (pred[2,384,768]{2,1,0:T(32,128)(4,1)}, pred[2,384,768]{2,1,0:T(32,128)(4,1)S(1)}, u32[]{:S(2)}) copy-start(pred[2,384,768]{2,1,0:T(32,128)(4,1)S(1)} %and_convert_fusion.7) | copy-start | bytes 1769476
  625.2 195.1 %copy-start.132 = (pred[2,384,768]{2,1,0:T(32,128)(4,1)}, pred[2,384,768]{2,1,0:T(32,128)(4,1)S(1)}, u32[]{:S(2)}) copy-start(pred[2,384,768]{2,1,0:T(32,128)(4,1)S(1)} %and_convert_fusion.6) | copy-start | bytes 1769476
  714.9 89.8 %all-to-all-start.2 = ((f32[16,48,1280]{2,1,0:T(8,128)}), f32[16,48,1280]{2,1,0:T(8,128)}, u32[]{:S(2)}, u32[]{:S(2)}) async-start(f32[16,48,1280]{2,1,0:T(8,128)} %bitcast.664), calls=%async_computation.4 | async-start | bytes 7864320 | tf_op jit(solution)/shard_map/all_to_all | solution.py:261
  826.5 54.1 %all-to-all-start.4 = ((f32[16,48,1280]{2,1,0:T(8,128)}), f32[16,48,1280]{2,1,0:T(8,128)}, u32[]{:S(2)}, u32[]{:S(2)}) async-start(f32[16,48,1280]{2,1,0:T(8,128)} %bitcast.663), calls=%async_computation.6 | async-start | bytes 7864320 | tf_op jit(solution)/shard_map/all_to_all | solution.py:261
  830.4 401.6 %reduce-scatter.11.cloned.1.call-start = ((), (), s32[]{:S(2)}) async-start(), calls=%async_computation.15 | async-start | bytes 30081024 | tf_op jit(solution)/shard_map/reduce_scatter | solution.py:258
  890.7 34.4 %copy-start.118 = (bf16[2,12,64,384]{3,2,1,0:T(8,128)(2,1)}, bf16[2,12,64,384]{3,2,1,0:T(8,128)(2,1)S(1)}, u32[]{:S(2)}) copy-start(bf16[2,12,64,384]{3,2,1,0:T(8,128)(2,1)S(1)} %get-tuple-element.268) | copy-start | bytes 3538948
  890.8 21.0 %slice-start.2 = ((s8[14155776]{0:T(1024)(128)(4,1)}), s8[1572864]{0:T(1024)(128)(4,1)S(1)}, s32[]{:S(2)}) async-start(s8[14155776]{0:T(1024)(128)(4,1)} %bitcast.608), calls=%async_computation.22 | async-start | bytes 3145728
  941.9 23.1 %copy-start.64 = (bf16[16,48,768]{2,1,0:T(8,128)(2,1)S(1)}, bf16[16,48,768]{2,1,0:T(8,128)(2,1)}, u32[]{:S(2)}) copy-start(bf16[16,48,768]{2,1,0:T(8,128)(2,1)} %get-tuple-element.179) | copy-start | bytes 3538948
  941.9 331.5 %reduce-scatter.9.cloned.1.call-start = ((), (), s32[]{:S(2)}) async-start(), calls=%async_computation.14 | async-start | bytes 31752192 | tf_op jit(solution)/shard_map/reduce_scatter | solution.py:258
  1118.3 34.7 %all-to-all-start.5 = ((f32[16,48,768]{2,1,0:T(8,128)}), f32[16,48,768]{2,1,0:T(8,128)}, u32[]{:S(2)}, u32[]{:S(2)}) async-start(f32[16,48,768]{2,1,0:T(8,128)} %bitcast.156), calls=%async_computation.7 | async-start | bytes 4718592 | tf_op jit(solution)/shard_map/all_to_all | solution.py:261
  1304.1 47.2 %copy-start.209 = (f32[3,2,624]{2,1,0:T(2,128)S(1)}, f32[3,2,624]{2,1,0:T(2,128)}, u32[]{:S(2)}) copy-start(f32[3,2,624]{2,1,0:T(2,128)} %param.18) | copy-start | bytes 44932
  (279 other events, 1069.6 us)
Sparse Core Ops, SparseCore 0:
  13.7 39.5 all-gather.18
  56.2 39.3 all-gather.14
  98.4 61.1 all-gather.16
  162.3 79.2 all-gather.20
  333.8 53.2 all-gather.10
  389.8 52.0 all-gather.12
  490.6 124.8 reduce-scatter.4
  621.0 143.2 reduce-scatter.6
  942.0 152.8 reduce-scatter.10
  1114.8 158.4 reduce-scatter.8

commit v3 on v2

--- a/solution.py
+++ b/solution.py
@@ -20,6 +20,7 @@
 TOKEN_TILE = 512
 VOCAB_TILE = 512
 GRAD_TILE = 640
+GRAD_TOKENS = 1024
 VMEM_BYTES = 60 * 1024 * 1024
 
 
@@ -223,15 +224,15 @@
     slice_len = head_t.shape[1]
     width = slice_len // 2
     whole = pl.BlockSpec((d_model, width), lambda i: (0, 0))
-    row = pl.BlockSpec((1, TOKEN_TILE), lambda i: (0, i))
+    row = pl.BlockSpec((1, GRAD_TOKENS), lambda i: (0, i))
     extra = () if init is None else (init,)
     return pl.pallas_call(
         functools.partial(head_grad_kernel, inv_tokens, half * width),
-        grid=(tokens // TOKEN_TILE,),
+        grid=(tokens // GRAD_TOKENS,),
         out_shape=jax.ShapeDtypeStruct((d_model, width), jnp.float32),
-        in_specs=[pl.BlockSpec((TOKEN_TILE, d_model), lambda i: (i, 0)), pl.BlockSpec((d_model, width), lambda i: (0, half)), pl.BlockSpec((1, width), lambda i: (0, half)), row, row] + [whole] * len(extra),
+        in_specs=[pl.BlockSpec((GRAD_TOKENS, d_model), lambda i: (i, 0)), pl.BlockSpec((d_model, width), lambda i: (0, half)), pl.BlockSpec((1, width), lambda i: (0, half)), row, row] + [whole] * len(extra),
         out_specs=whole,
-        scratch_shapes=[pltpu.VMEM((d_model, TOKEN_TILE), jnp.bfloat16)],
+        scratch_shapes=[pltpu.VMEM((d_model, GRAD_TOKENS), jnp.bfloat16)],
         compiler_params=pltpu.CompilerParams(vmem_limit_bytes=VMEM_BYTES, dimension_semantics=('arbitrary',)),
         cost_estimate=pl.CostEstimate(flops=4 * tokens * d_model * width, bytes_accessed=tokens * d_model * 2 + head_t.size * 3, transcendentals=tokens * width),
     )(h_all, head_t, mask, lse, tgt, *extra)
@@ -281,7 +282,7 @@
         head_send = jnp.pad(st_wte[0].T.astype(jnp.bfloat16), ((0, 0), (0, vocab_pad - vocab_size)))
         head_send = jnp.swapaxes(head_send.reshape(shard, n_dev, slice_len), 0, 1)
         ids_all = lax.all_gather(jnp.stack([token_ids, target_ids]), 'dp', axis=1, tiled=True).reshape(2, tokens)
-        token_send, target_send = lookup_rows(ids_all, head_send, tok_dev)
+        token_send, = lookup_rows(ids_all[:1], head_send, tok_dev)
         token_rows = swap(token_send).reshape(d_model, tok_dev).T.astype(jnp.float32)
 
         def half_pack(parts):
@@ -328,6 +329,9 @@
         mask = jnp.where(vocab_pos < vocab_size, 0.0, -1e30).astype(jnp.float32)
         tgt_local = (ids_all[1] - me * slice_len).astype(jnp.float32).reshape(n_dev, batch_dev, seq_len)
         h_alls = [gather(normed[row]).reshape(n_dev * seq_len, d_model) for row in range(batch_dev)]
+        late_ids, _ = lax.optimization_barrier((ids_all[1:], normed))
+        target_send, = lookup_rows(late_ids, head_send, tok_dev)
+        head_t, target_send = lax.optimization_barrier((head_t, target_send))
         target_rows = swap(target_send).reshape(d_model, tok_dev).T.astype(jnp.float32).reshape(batch_dev, seq_len, d_model)
         lse_alls, d_sums, loss_part = [], [], 0.0
         for row in range(batch_dev):
@@ -357,7 +361,7 @@
         d_normed = jnp.stack(d_sums) - inv_tokens * target_rows
 
         d_resid, d_lnf = norm_back(d_normed.astype(jnp.bfloat16))
-        vec_rows = [None] * num_layers
+        vec_rows, packed_sums = [None] * num_layers, []
         qkv_g, proj_g, up_g, down_g = ([None] * num_layers for _ in range(4))
         feed_rows = attn_rows + ff_parts * shard
         for layer in reversed(range(num_layers)):
@@ -376,6 +380,7 @@
                 rows = jnp.pad(rows, ((0, 0), (0, (-(num_layers + 1 + pos_count)) % 8), (0, d_model - vec_shard)))
                 parts = parts + [pos_sum, rows]
             summed = scatter_sum(jnp.concatenate(parts, axis=1))
+            packed_sums.append(summed)
             qkv_g[layer] = jnp.swapaxes(summed[:3 * shard].reshape(3, shard, d_model), 0, 1).reshape(st_qkv.shape[2:])
             proj_g[layer] = summed[3 * shard:attn_rows].T.reshape(st_proj.shape[2:])
             up_g[layer] = jnp.swapaxes(summed[attn_rows:feed_rows].reshape(ff_parts, shard, d_model), 0, 1).reshape(shard, ff_dim)
@@ -390,9 +395,9 @@
         lookup_d = swap(d_resid.reshape(tok_dev, d_model).T.reshape(n_dev, shard, tok_dev))
         wte_g, wte_sq = accumulate_rows(ids_all, lookup_d, grad_heads)
 
+        local_sq = jnp.sum(wte_sq) + sum(jnp.sum(summed * summed) for summed in packed_sums)
         grads = [pos_g, jnp.stack(qkv_g), jnp.stack(proj_g), jnp.stack(up_g), jnp.stack(down_g), vec_g, lnf_g]
-        local_sq = jnp.sum(wte_sq) + sum(jnp.sum(grad * grad) for grad in grads)
-        sums = lax.psum(jnp.stack([local_sq, loss_part]), 'dp')
+        sums = jnp.sum(gather(jnp.pad(jnp.stack([local_sq, loss_part]), (0, LANES - 2))), axis=0)
         clip_coef = jnp.minimum(1.0, CLIP_NORM / (jnp.sqrt(sums[0]) + 1e-6))
         new_wte = jnp.swapaxes(adam_update(jnp.swapaxes(st_wte, 1, 2), wte_g[:, :vocab_size] * clip_coef, DECAYS[0]), 1, 2)
         states = (st_wpe, st_qkv, st_proj, st_up, st_down, st_vec, st_lnf)

time: 1420 us -> 1360 us (0.958)
  local copies, waits for them, and re-layouts: 235 us -> 207 us
  waiting for transfers between devices: 168 us -> 195 us
  Pallas kernels: 466 us -> 440 us
  blocking collectives: 74.1 us -> 54.2 us
    psum x1 -> x0, blocking collectives: 32.3 us -> none  [train_step(): sums = lax.psum(jnp.stack([local_sq, loss_part]), 'dp')]
    all_gather x6, waiting for transfers between devices: 52.3 us -> 77.4 us  [gather(): return lax.all_gather(local, 'dp', axis=0, tiled=False)]
    pallas_call x1 -> x2, Pallas kernels: 64.2 us -> 42.9 us  [lookup_rows(): pl.pallas_call(lookup_kernel, out_shape=[jax.ShapeDtypeStruct((parts, sha...]
    all_gather x2 -> x3, blocking collectives: 26.9 us -> 39.3 us  [gather(): return lax.all_gather(local, 'dp', axis=0, tiled=False)]
  transfers between devices with their start and end apart: 16 -> 16, of which waited for: 6 -> 8; matrix products, arithmetic and copies ran while one was open for 27% -> 27% of each run, Pallas kernels for 33% -> 33%
where the time goes in v3:
time: 1360 us; the launch traced here: 1350 us
  Pallas kernels  440 us (32%)
  matrix products  226 us (17%)
  local copies, waits for them, and re-layouts  207 us (15%)
  waiting for transfers between devices  195 us (14%)
  other arithmetic  179 us (13%)
  blocking collectives  54.2 us (4%)
  between operations  22.9 us (2%)
  starting transfers between devices  21.8 us (2%)
    pallas_call x4, Pallas kernels, head_grad(): pl.pallas_call(functools.partial(head_grad_kernel, inv_tokens, half * wid...  167 us
    pallas_call x2, Pallas kernels, head_forward(): pl.pallas_call(head_forward_kernel, grid=(tokens // TOKEN_TILE,), out_sha...  152 us
    dot_general x42, matrix products, affine(): jnp.einsum('bsd,de->bse', x, weight, preferred_element_type=jnp.float32)  84.4 us
    all_to_all x6, waiting for transfers between devices, swap(): lax.all_to_all(blocks, 'dp', split_axis=0, concat_axis=0, tiled=False)  83 us
    pallas_call x1, Pallas kernels, accumulate_rows(): pl.pallas_call(accumulate_kernel, out_shape=(jax.ShapeDtypeStruct((shard,...  77.7 us
    all_gather x6, waiting for transfers between devices, gather(): return lax.all_gather(local, 'dp', axis=0, tiled=False)  77.4 us
    unnamed x610, local copies, waits for them, and re-layouts  61.2 us
    pallas_call x2, Pallas kernels, lookup_rows(): pl.pallas_call(lookup_kernel, out_shape=[jax.ShapeDtypeStruct((parts, sha...  42.9 us
  transfers between devices with their start and end apart: 16, of which 8 were waited for; matrix products, arithmetic and copies ran while one was open for 27% of the time, Pallas kernels for 33%

profile of v3, /device:TPU:0, one launch (start us, length us, event | category | flops | bytes accessed | tf_op | source)
XLA Modules:
  0.0 1347.1 jit_solution(10903292284835082551)
XLA Ops:
  43.8 14.9 %all_gather.45 = s32[2,32,384]{2,0,1:T(2,128)S(1)} all-gather(s32[2,2,384]{2,0,1:T(2,128)S(1)} %pad_add_fusion), channel_id=1, replica_groups=mesh['dp'=16] {'dp'}, dimensions={1}, use_global_device_ids=true | all-gather | bytes 104448 | tf_op jit(solution)/shard_map/all_gather | solution.py:284
  60.1 21.4 %shard_map.169 = bf16[16,48,768]{2,1,0:T(8,128)(2,1)} custom-call(s32[1,12288]{1,0:T(1,128)} %bitcast.761, bf16[16,48,2560]{2,1,0:T(8,128)(2,1)} %bitcast.618), custom_call_target="tpu_custom_call" | custom-call | flops 30000001024 | bytes 5111808 | tf_op jit(solution)/shard_map/pallas_call | solution.py:99
  84.6 24.5 %all-to-all-done = bf16[16,48,768]{2,1,0:T(8,128)(2,1)S(1)} async-done(((bf16[16,48,768]{2,1,0:T(8,128)(2,1)}), bf16[16,48,768]{2,1,0:T(8,128)(2,1)S(1)}, u32[]{:S(2)}, u32[]{:S(2)}) %all-to-all-start) | async-done | bytes 1179680 | tf_op jit(solution)/shard_map/all_to_all | solution.py:262
  158.5 9.8 fusion.233
  168.3 9.7 divide_convert_fusion.1
  186.1 11.0 all-gather.19.cloned.1.call-done
  215.0 36.8 %all-gather.23.cloned.1.call-done = bf16[6144,768]{1,0:T(8,128)(2,1)} async-done(((bf16[384,768]{1,0:T(8,128)(2,1)}), bf16[6144,768]{1,0:T(8,128)(2,1)}) %all-gather.23.cloned.1.call-update) | async-done | bytes 9437200 | tf_op jit(solution)/shard_map/all_gather | solution.py:256
  288.6 9.7 fusion.235
  298.3 9.6 divide_convert_fusion
  335.9 21.4 %shard_map.170 = bf16[16,48,768]{2,1,0:T(8,128)(2,1)} custom-call(s32[1,12288]{1,0:T(1,128)} %bitcast.760, bf16[16,48,2560]{2,1,0:T(8,128)(2,1)} %bitcast.620), custom_call_target="tpu_custom_call" | custom-call | flops 30000001024 | bytes 5111808 | tf_op jit(solution)/shard_map/pallas_call | solution.py:99
  357.3 29.6 %all-gather.13.cloned.1.call-done = bf16[16,384,768]{2,1,0:T(8,128)(2,1)} async-done(((bf16[1,384,768]{2,1,0:T(8,128)(2,1)}), bf16[16,384,768]{2,1,0:T(8,128)(2,1)}) %all-gather.13.cloned.1.call-update) | async-done | bytes 9437200 | tf_op jit(solution)/shard_map/all_gather | solution.py:256
  386.8 76.0 %shard_map.171 = (f32[6144,768]{1,0:T(8,128)}, f32[8,6144]{1,0:T(8,128)}) custom-call(bf16[6144,768]{1,0:T(8,128)(2,1)} %bitcast.767, bf16[768,2560]{1,0:T(8,128)(2,1)} %bitcast.96.head_ref, f32[1,2560]{1,0:T(1,128)} %compare_select_fusion.mask_ref), custom_call_target="tpu_custom_call" | custom-call | flops 48318382080 | bytes 32243712 | tf_op jit(solution)/shard_map/pallas_call | solution.py:185
  463.9 13.4 all_gather.55
  477.5 12.6 broadcast_multiply_fusion.1
  490.2 76.3 %shard_map.172 = (f32[6144,768]{1,0:T(8,128)}, f32[8,6144]{1,0:T(8,128)}) custom-call(bf16[6144,768]{1,0:T(8,128)(2,1)} %bitcast.770, bf16[768,2560]{1,0:T(8,128)(2,1)} %bitcast.96.head_ref, f32[1,2560]{1,0:T(1,128)} %compare_select_fusion.mask_ref), custom_call_target="tpu_custom_call" | custom-call | flops 48318382080 | bytes 32243712 | tf_op jit(solution)/shard_map/pallas_call | solution.py:185
  567.5 13.5 all_gather.57
  581.2 12.8 broadcast_multiply_fusion
  603.5 14.3 %all-to-all-done.3 = bf16[16,48,768]{2,1,0:T(8,128)(2,1)S(1)} async-done(((bf16[16,48,768]{2,1,0:T(8,128)(2,1)}), bf16[16,48,768]{2,1,0:T(8,128)(2,1)S(1)}, u32[]{:S(2)}, u32[]{:S(2)}) %all-to-all-start.3) | async-done | bytes 1179680 | tf_op jit(solution)/shard_map/all_to_all | solution.py:262
  621.5 41.7 %shard_map.173.refs_0_ = f32[768,1280]{1,0:T(8,128)} custom-call(bf16[6144,768]{1,0:T(8,128)(2,1)} %bitcast.768, bf16[768,2560]{1,0:T(8,128)(2,1)} %bitcast.96.head_ref, f32[1,2560]{1,0:T(1,128)} %compare_select_fusion.mask_ref, f32[1,6144]{1,0:T(1,128)} %bitcast.754, f32[1,6144]{1,0:T(1,128)} %bitcast.764), custom_call_target="tpu_custom_call" | custom-call | flops 24159191040 | bytes 15335424 | tf_op jit(solution)/shard_map/pallas_call | solution.py:229
  663.3 42.2 %shard_map.174 = f32[768,1280]{1,0:T(8,128)} custom-call(bf16[6144,768]{1,0:T(8,128)(2,1)} %bitcast.771, bf16[768,2560]{1,0:T(8,128)(2,1)} %bitcast.96.head_ref, f32[1,2560]{1,0:T(1,128)} %compare_select_fusion.mask_ref, f32[1,6144]{1,0:T(1,128)} %bitcast.756, f32[1,6144]{1,0:T(1,128)} %bitcast.762, f32[768,1280]{1,0:T(8,128)} %shard_map.173.refs_0_), custom_call_target="tpu_custom_call" | custom-call | flops 24159191040 | bytes 15335424 | tf_op jit(solution)/shard_map/pallas_call | solution.py:229
  709.0 40.9 %shard_map.175.refs_0_ = f32[768,1280]{1,0:T(8,128)} custom-call(bf16[6144,768]{1,0:T(8,128)(2,1)} %bitcast.769, bf16[768,2560]{1,0:T(8,128)(2,1)} %bitcast.96.head_ref, f32[1,2560]{1,0:T(1,128)} %compare_select_fusion.mask_ref, f32[1,6144]{1,0:T(1,128)} %bitcast.755, f32[1,6144]{1,0:T(1,128)} %bitcast.765), custom_call_target="tpu_custom_call" | custom-call | flops 24159191040 | bytes 15335424 | tf_op jit(solution)/shard_map/pallas_call | solution.py:229
  749.9 42.6 %shard_map.176 = f32[768,1280]{1,0:T(8,128)} custom-call(bf16[6144,768]{1,0:T(8,128)(2,1)} %bitcast.772, bf16[768,2560]{1,0:T(8,128)(2,1)} %bitcast.96.head_ref, f32[1,2560]{1,0:T(1,128)} %compare_select_fusion.mask_ref, f32[1,6144]{1,0:T(1,128)} %bitcast.757, f32[1,6144]{1,0:T(1,128)} %bitcast.763, f32[768,1280]{1,0:T(8,128)} %shard_map.175.refs_0_), custom_call_target="tpu_custom_call" | custom-call | flops 24159191040 | bytes 15335424 | tf_op jit(solution)/shard_map/pallas_call | solution.py:229
  841.6 26.7 %all-to-all-done.4.high_ref = f32[16,48,1280]{2,1,0:T(8,128)} async-done(((f32[16,48,1280]{2,1,0:T(8,128)}), f32[16,48,1280]{2,1,0:T(8,128)}, u32[]{:S(2)}, u32[]{:S(2)}) %all-to-all-start.4) | async-done | bytes 3932192 | tf_op jit(solution)/shard_map/all_to_all | solution.py:262
  887.1 12.5 convert_reduce_fusion.6
  919.9 9.8 concatenate.89
  987.3 8.7 fusion.13
  996.1 10.6 convert_reduce_fusion.9
  1123.5 17.4 %all-to-all-done.5.d_ref = f32[16,48,768]{2,1,0:T(8,128)} async-done(((f32[16,48,768]{2,1,0:T(8,128)}), f32[16,48,768]{2,1,0:T(8,128)}, u32[]{:S(2)}, u32[]{:S(2)}) %all-to-all-start.5) | async-done | bytes 2359328 | tf_op jit(solution)/shard_map/all_to_all | solution.py:262
  1140.9 77.7 %shard_map.177 = (f32[48,40960]{1,0:T(8,128)}, f32[48,128]{1,0:T(8,128)}) custom-call(s32[2,12288]{1,0:T(2,128)} %bitcast.749, f32[16,48,768]{2,1,0:T(8,128)} %all-to-all-done.5.d_ref, f32[16,48,1280]{2,1,0:T(8,128)} %all-to-all-done.2.low_ref, f32[16,48,1280]{2,1,0:T(8,128)} %all-to-all-done.4.high_ref), custom_call_target="tpu_custom_call" | custom-call | flops 49999998976 | bytes 18087936 | tf_op jit(solution)/shard_map/pallas_call | solution.py:147
  1227.9 33.4 %reduce-scatter.11.cloned.1.call-done = f32[1,608,768]{2,1,0:T(8,128)} async-done(((f32[16,608,768]{2,1,0:T(8,128)}), f32[1,608,768]{2,1,0:T(8,128)}) %reduce-scatter.11.cloned.1.call-update) | async-done | bytes 1867792 | tf_op jit(solution)/shard_map/reduce_scatter | solution.py:259
  1266.0 12.5 all-gather.5
  1304.4 16.2 %fusion.22 = (f32[1,48,40478]{2,1,0:T(8,128)S(1)}, f32[1,48,40478]{2,1,0:T(8,128)S(1)}, f32[1,48,40478]{2,1,0:T(8,128)}) fusion(f32[3,48,40478]{2,1,0:T(8,128)} %bitcast.612, f32[]{:T(128)} %bitcast.228, f32[48,40960]{1,0:T(8,128)} %get-tuple-element.48), kind=kLoop, calls=%fused_computation.40 | loop fusion | flops 27201216 | bytes 54402436 | tf_op jit(solution)/shard_map/stack | solution.py:247
  (964 shorter events, 513.7 us)
Async XLA Ops:
  7.2 109.2 %all-gather.21.cloned.1.call-start = ((), (), s32[]{:S(2)}) async-start(), calls=%async_computation.18 | async-start | bytes 5013504 | tf_op jit(solution)/shard_map/all_gather | solution.py:256
  13.6 108.2 %all-gather.17.cloned.1.call-start = ((), (), s32[]{:S(2)}) async-start(), calls=%async_computation.16 | async-start | bytes 5849088 | tf_op jit(solution)/shard_map/all_gather | solution.py:256
  33.7 163.4 %all-gather.19.cloned.1.call-start = ((), (), s32[]{:S(2)}) async-start(), calls=%async_computation.17 | async-start | bytes 10027008 | tf_op jit(solution)/shard_map/all_gather | solution.py:256
  36.9 214.9 %all-gather.23.cloned.1.call-start = ((), (), s32[]{:S(2)}) async-start(), calls=%async_computation.19 | async-start | bytes 10027008 | tf_op jit(solution)/shard_map/all_gather | solution.py:256
  81.5 27.7 %all-to-all-start = ((bf16[16,48,768]{2,1,0:T(8,128)(2,1)}), bf16[16,48,768]{2,1,0:T(8,128)(2,1)S(1)}, u32[]{:S(2)}, u32[]{:S(2)}) async-start(bf16[16,48,768]{2,1,0:T(8,128)(2,1)} %shard_map.169), calls=%async_computation | async-start | bytes 2359296 | tf_op jit(solution)/shard_map/all_to_all | solution.py:262
  109.2 160.1 %all-to-all-start.1 = ((bf16[16,48,2560]{2,1,0:T(8,128)(2,1)}), bf16[16,48,2560]{2,1,0:T(8,128)(2,1)}, u32[]{:S(2)}, u32[]{:S(2)}) async-start(bf16[16,48,2560]{2,1,0:T(8,128)(2,1)} %bitcast.619), calls=%async_computation.1 | async-start | bytes 7864320 | tf_op jit(solution)/shard_map/all_to_all | solution.py:262
  112.4 274.4 %all-gather.13.cloned.1.call-start = ((), (), s32[]{:S(2)}) async-start(), calls=%async_computation.10 | async-start | bytes 10027008 | tf_op jit(solution)/shard_map/all_gather | solution.py:256
  116.4 66.4 %copy-start.2 = (f32[768,768]{0,1:T(8,128)}, f32[768,768]{0,1:T(8,128)S(1)}, u32[]{:S(2)}) copy-start(f32[768,768]{0,1:T(8,128)S(1)} %copy.249) | copy-start | bytes 7077892
  129.0 53.7 %copy-start.11 = (f32[768,384]{0,1:T(8,128)}, f32[768,384]{0,1:T(8,128)S(1)}, u32[]{:S(2)}) copy-start(f32[768,384]{0,1:T(8,128)S(1)} %copy.252) | copy-start | bytes 3538948
  131.4 54.2 %copy-start.176 = (f32[768]{0:T(1024)}, f32[768]{0:T(1024)S(1)}, u32[]{:S(2)}) copy-start(f32[768]{0:T(1024)S(1)} %get-tuple-element.116) | copy-start | bytes 9220
  156.6 176.0 %copy-start.186 = (f32[768]{0:T(1024)}, f32[768]{0:T(1024)S(1)}, u32[]{:S(2)}) copy-start(f32[768]{0:T(1024)S(1)} %mul.1026) | copy-start | bytes 9220
  158.5 112.1 %copy-start.182 = (f32[768]{0:T(1024)}, f32[768]{0:T(1024)S(1)}, u32[]{:S(2)}) copy-start(f32[768]{0:T(1024)S(1)} %get-tuple-element.110) | copy-start | bytes 9220
  158.5 155.5 %copy-start.184 = (f32[768]{0:T(1024)}, f32[768]{0:T(1024)S(1)}, u32[]{:S(2)}) copy-start(f32[768]{0:T(1024)S(1)} %get-tuple-element.103) | copy-start | bytes 9220
  215.0 48.4 %copy-start.74 = (bf16[4,192,768]{2,1,0:T(8,128)(2,1)}, bf16[4,192,768]{2,1,0:T(8,128)(2,1)S(1)}, u32[]{:S(2)}) copy-start(bf16[4,192,768]{2,1,0:T(8,128)(2,1)S(1)} %get-tuple-element.169) | copy-start | bytes 3538948
  215.0 50.6 %copy-start.72 = (bf16[4,192,768]{2,1,0:T(8,128)(2,1)}, bf16[4,192,768]{2,1,0:T(8,128)(2,1)S(1)}, u32[]{:S(2)}) copy-start(bf16[4,192,768]{2,1,0:T(8,128)(2,1)S(1)} %get-tuple-element.170) | copy-start | bytes 3538948
  215.0 51.8 %copy-start.37 = (bf16[4,192,768]{2,1,0:T(8,128)(2,1)}, bf16[4,192,768]{2,1,0:T(8,128)(2,1)S(1)}, u32[]{:S(2)}) copy-start(bf16[4,192,768]{2,1,0:T(8,128)(2,1)S(1)} %get-tuple-element.167) | copy-start | bytes 3538948
  269.2 43.0 %copy-start = (f32[2,384,768]{2,1,0:T(8,128)}, f32[2,384,768]{2,1,0:T(8,128)S(1)}, u32[]{:S(2)}) copy-start(f32[2,384,768]{2,1,0:T(8,128)S(1)} %add_add_fusion.11) | copy-start | bytes 7077892
  334.6 155.5 %all-gather.15.cloned.1.call-start = ((), (), s32[]{:S(2)}) async-start(), calls=%async_computation.11 | async-start | bytes 10027008 | tf_op jit(solution)/shard_map/all_gather | solution.py:256
  335.2 457.3 %reduce-scatter.5.cloned.1.call-start = ((), (), s32[]{:S(2)}) async-start(), calls=%async_computation.12 | async-start | bytes 20054016 | tf_op jit(solution)/shard_map/reduce_scatter | solution.py:259
  490.1 302.4 %reduce-scatter.7.cloned.1.call-start = ((), (), s32[]{:S(2)}) async-start(), calls=%async_computation.13 | async-start | bytes 20054016 | tf_op jit(solution)/shard_map/reduce_scatter | solution.py:259
  595.7 22.1 %all-to-all-start.3 = ((bf16[16,48,768]{2,1,0:T(8,128)(2,1)}), bf16[16,48,768]{2,1,0:T(8,128)(2,1)S(1)}, u32[]{:S(2)}, u32[]{:S(2)}) async-start(bf16[16,48,768]{2,1,0:T(8,128)(2,1)} %shard_map.170), calls=%async_computation.5 | async-start | bytes 2359296 | tf_op jit(solution)/shard_map/all_to_all | solution.py:262
  600.1 206.8 %copy-start.131 = (pred[2,384,768]{2,1,0:T(32,128)(4,1)}, pred[2,384,768]{2,1,0:T(32,128)(4,1)S(1)}, u32[]{:S(2)}) copy-start(pred[2,384,768]{2,1,0:T(32,128)(4,1)S(1)} %and_convert_fusion.7) | copy-start | bytes 1769476
  600.8 207.3 %copy-start.133 = (pred[2,384,768]{2,1,0:T(32,128)(4,1)}, pred[2,384,768]{2,1,0:T(32,128)(4,1)S(1)}, u32[]{:S(2)}) copy-start(pred[2,384,768]{2,1,0:T(32,128)(4,1)S(1)} %and_convert_fusion.6) | copy-start | bytes 1769476
  621.5 172.8 %copy-start.13 = (f32[768,768]{0,1:T(8,128)}, f32[768,768]{0,1:T(8,128)S(1)}, u32[]{:S(2)}) copy-start(f32[768,768]{0,1:T(8,128)S(1)} %copy.267) | copy-start | bytes 7077892
  705.5 87.0 %all-to-all-start.2 = ((f32[16,48,1280]{2,1,0:T(8,128)}), f32[16,48,1280]{2,1,0:T(8,128)}, u32[]{:S(2)}, u32[]{:S(2)}) async-start(f32[16,48,1280]{2,1,0:T(8,128)} %bitcast.654), calls=%async_computation.4 | async-start | bytes 7864320 | tf_op jit(solution)/shard_map/all_to_all | solution.py:262
  814.3 54.0 %all-to-all-start.4 = ((f32[16,48,1280]{2,1,0:T(8,128)}), f32[16,48,1280]{2,1,0:T(8,128)}, u32[]{:S(2)}, u32[]{:S(2)}) async-start(f32[16,48,1280]{2,1,0:T(8,128)} %bitcast.653), calls=%async_computation.6 | async-start | bytes 7864320 | tf_op jit(solution)/shard_map/all_to_all | solution.py:262
  818.2 401.8 %reduce-scatter.9.cloned.1.call-start = ((), (), s32[]{:S(2)}) async-start(), calls=%async_computation.14 | async-start | bytes 30081024 | tf_op jit(solution)/shard_map/reduce_scatter | solution.py:259
  878.5 34.4 %copy-start.117 = (bf16[2,12,64,384]{3,2,1,0:T(8,128)(2,1)}, bf16[2,12,64,384]{3,2,1,0:T(8,128)(2,1)S(1)}, u32[]{:S(2)}) copy-start(bf16[2,12,64,384]{3,2,1,0:T(8,128)(2,1)S(1)} %get-tuple-element.270) | copy-start | bytes 3538948
  929.8 331.5 %reduce-scatter.11.cloned.1.call-start = ((), (), s32[]{:S(2)}) async-start(), calls=%async_computation.15 | async-start | bytes 31752192 | tf_op jit(solution)/shard_map/reduce_scatter | solution.py:259
  1106.3 34.6 %all-to-all-start.5 = ((f32[16,48,768]{2,1,0:T(8,128)}), f32[16,48,768]{2,1,0:T(8,128)}, u32[]{:S(2)}, u32[]{:S(2)}) async-start(f32[16,48,768]{2,1,0:T(8,128)} %bitcast.158), calls=%async_computation.7 | async-start | bytes 4718592 | tf_op jit(solution)/shard_map/all_to_all | solution.py:262
  1224.6 55.3 %copy-start.212 = (f32[3,2,624]{2,1,0:T(2,128)S(1)}, f32[3,2,624]{2,1,0:T(2,128)}, u32[]{:S(2)}) copy-start(f32[3,2,624]{2,1,0:T(2,128)} %param.18) | copy-start | bytes 44932
  1224.6 58.3 %copy-start.142 = (f32[3,514,48]{1,2,0:T(8,128)S(1)}, f32[3,514,48]{1,2,0:T(8,128)}, u32[]{:S(2)}) copy-start(f32[3,514,48]{1,2,0:T(8,128)} %param.13) | copy-start | bytes 888196
  (279 other events, 1149.3 us)
Sparse Core Ops, SparseCore 0:
  13.7 39.5 all-gather.20
  56.2 50.3 all-gather.16
  109.4 87.6 all-gather.18
  199.7 52.0 all-gather.22
  334.7 52.0 all-gather.12
  388.9 52.0 all-gather.14
  490.3 119.6 reduce-scatter.4
  615.4 145.3 reduce-scatter.6
  929.9 152.8 reduce-scatter.8
  1102.8 158.4 reduce-scatter.10
